TPU v7x, 512 devices: a whole 4x8x8 slice. The times are simulated.
512 devices in a mesh: outer: 16 (over x, y_lo), inner: 32 (over z, y_hi, core).
Axes of the slice: x: 4, y: 8 (y_hi: 2, y_lo: 4; y = y_hi * 4 + y_lo), z: 8, core: 2. Of those that a mesh axis runs over, the one named last changes fastest.
Arguments:
- queries: bfloat16 [131072, 512], P(('outer', 'inner')), may hold values from -56 to 56
- keys: bfloat16 [131072, 512], P(('outer', 'inner')), may hold values from -48 to 48
- values: bfloat16 [131072, 512], P(('outer', 'inner')), may hold values from -6 to 6
- out_weight: bfloat16 [512, 768], replicated, may hold values from -0.25 to 0.25
- slide_lengths: int32 [16], replicated, may hold values from 1 to 98304, 131072 in all
Outputs:
- mixed_output: bfloat16 [131072, 768], P(('outer', 'inner'))
Inputs may be any that keep to these rules, and one draw needn't show every extreme that they name: `slide_lengths`: the lengths sum to 131072.
All inputs are finite; a program needn't handle non-finite values.
Results may differ from a plain program's by a relative error of at most 0.0052.
Values may be sent and summed in bfloat16 or wider, within the bound.
A program may use at most 64 MiB of HBM per device.

v0:
```python
import jax
import jax.numpy as jnp
from jax import lax
from jax.sharding import PartitionSpec as P

HEADS = 8
HEAD_DIM = 64
SPARSE = 1024


masked_score = -1e30


def from_partner(block, axis, distance):
    count = lax.axis_size(axis)
    route = []
    for low in range(count):
        high = low | 1 << distance
        if high != low and high < count:
            route += [(low, high), (high, low)]
    return lax.ppermute(block, axis, route)


def sent_together(arrays, axis, split_dim, concat_dim, along):
    both = jnp.concatenate(arrays, axis=along)
    filled, at, outs = (
        lax.all_to_all(both, axis, split_axis=split_dim, concat_axis=concat_dim, tiled=True),
        0,
        [],
    )
    for a in arrays:
        outs.append(lax.slice_in_dim(filled, at, at + a.shape[along], axis=along))
        at += a.shape[along]
    return tuple(outs)


def sent_together_2(arrays, axis, dim, along):
    both = jnp.concatenate(arrays, axis=along)
    filled, at, outs = (lax.all_gather(both, axis, axis=dim, tiled=True), 0, [])
    for a in arrays:
        outs.append(lax.slice_in_dim(filled, at, at + a.shape[along], axis=along))
        at += a.shape[along]
    return tuple(outs)


def slide_index(positions, slide_ends):
    return jnp.sum((positions[:, None] >= slide_ends[None, :]).astype(jnp.int32), axis=1)


def segment_attention(query_rows, key_rows, value_rows, query_slides, key_slides):
    scores = jnp.dot(query_rows, key_rows.T, preferred_element_type=jnp.float32) * HEAD_DIM ** (
        -0.5
    )
    scores = jnp.where(query_slides[:, None] == key_slides[None, :], scores, masked_score)
    row_max = jnp.max(scores, axis=1, keepdims=True)
    expos = jnp.exp(scores - row_max)
    totals = jnp.sum(expos, axis=1, keepdims=True)
    probs = expos.astype(jnp.bfloat16)
    branch = jnp.dot(probs, value_rows, preferred_element_type=jnp.float32) / totals
    return (branch, row_max[:, 0] + jnp.log(totals[:, 0]))


def mix_levels(first, second, third):
    largest = jnp.maximum(jnp.maximum(first[1], second[1]), third[1])
    weighted = jnp.zeros_like(first[0])
    weight_sum = jnp.zeros_like(first[1])
    for branch, branch_lse in (first, second, third):
        factor = jnp.exp(branch_lse - largest)
        weighted = weighted + factor[:, None] * branch
        weight_sum = weight_sum + factor
    return weighted / weight_sum[:, None]


def select_rows(matrix, step_rate):
    row_count = matrix.shape[0] // step_rate
    grouped = matrix.reshape(row_count, step_rate, HEADS, HEAD_DIM)
    picked = [grouped[:, head_index % step_rate, head_index, :] for head_index in range(HEADS)]
    return jnp.stack(picked, axis=1).reshape(row_count, HEADS * HEAD_DIM)


def spread_rows(branch, branch_lse, step_rate, offset):
    row_count = branch.shape[0]
    full_branch = jnp.zeros((row_count, step_rate, branch.shape[1]), jnp.float32)
    full_branch = (
        full_branch.at[:, offset, :].set(branch).reshape(row_count * step_rate, branch.shape[1])
    )
    full_lse = jnp.full((row_count, step_rate), masked_score, jnp.float32)
    full_lse = full_lse.at[:, offset].set(branch_lse).reshape(row_count * step_rate)
    return (full_branch, full_lse)


def head_slots(selected, group):
    row_count = selected.shape[0]
    per_head = selected.reshape(row_count, HEADS, HEAD_DIM).transpose(1, 0, 2)
    return jnp.repeat(per_head, group, axis=0)


def query_slots(queries, step_rate, group, first_token, slide_ends):
    selected = select_rows(queries, step_rate)
    row_count = selected.shape[0]
    per_slot = -(-row_count // group)
    padding = group * per_slot - row_count
    grouped = jnp.pad(selected.reshape(row_count, HEADS, HEAD_DIM), ((0, padding), (0, 0), (0, 0)))
    grouped = (
        grouped.reshape(group, per_slot, HEADS, HEAD_DIM)
        .transpose(2, 0, 1, 3)
        .reshape(HEADS * group, per_slot, HEAD_DIM)
    )
    head_offsets = jnp.arange(HEADS, dtype=jnp.int32) % step_rate
    positions = (
        first_token
        + jnp.arange(row_count, dtype=jnp.int32)[None, :] * step_rate
        + head_offsets[:, None]
    )
    slides = slide_index(positions.reshape(-1), slide_ends).reshape(HEADS, row_count)
    slides = jnp.pad(slides, ((0, 0), (0, padding))).reshape(HEADS * group, per_slot)
    return (grouped, slides, row_count)


def unslot(returned, row_count, group):
    branch, branch_lse = returned
    per_slot = branch.shape[1]
    branch = branch.reshape(HEADS, group * per_slot, HEAD_DIM)[:, :row_count, :]
    branch_lse = branch_lse.reshape(HEADS, group * per_slot)[:, :row_count]
    return (branch, branch_lse)


def shards(queries, keys, values, out_weight, slide_lengths):
    tok_dev = queries.shape[0]
    inner_count = lax.axis_size("inner")
    outer_count = lax.axis_size("outer")
    inner_index = lax.axis_index("inner")
    outer_index = lax.axis_index("outer")
    device_index = outer_index * inner_count + inner_index
    mid_rate = tok_dev * inner_count // SPARSE
    top_rate = mid_rate * outer_count
    local_group = SPARSE // tok_dev
    slide_ends = jnp.cumsum(slide_lengths)
    first_token = device_index * tok_dev
    mid_start = outer_index * tok_dev * inner_count
    local_keys = keys
    local_values = values
    for bit_index in range(local_group.bit_length() - 1):
        partner = from_partner((local_keys, local_values), "inner", bit_index)
        upper_half = inner_index // (1 << bit_index) % 2 == 1
        local_keys = jnp.concatenate(
            [
                jnp.where(upper_half, partner[0], local_keys),
                jnp.where(upper_half, local_keys, partner[0]),
            ],
            axis=0,
        )
        local_values = jnp.concatenate(
            [
                jnp.where(upper_half, partner[1], local_values),
                jnp.where(upper_half, local_values, partner[1]),
            ],
            axis=0,
        )
    local_start = first_token - inner_index % local_group * tok_dev
    local_levels = []
    for head_index in range(HEADS):
        columns = slice(head_index * HEAD_DIM, (head_index + 1) * HEAD_DIM)
        query_slides = slide_index(first_token + jnp.arange(tok_dev, dtype=jnp.int32), slide_ends)
        key_slides = slide_index(local_start + jnp.arange(SPARSE, dtype=jnp.int32), slide_ends)
        local_levels.append(
            segment_attention(
                queries[:, columns],
                local_keys[:, columns],
                local_values[:, columns],
                query_slides,
                key_slides,
            )
        )
    upper_levels = []
    group = inner_count // HEADS
    own_head = inner_index // group
    mid_keys_in, mid_values_in, top_keys_in, top_values_in = sent_together(
        (
            head_slots(select_rows(keys, mid_rate), group),
            head_slots(select_rows(values, mid_rate), group),
            head_slots(select_rows(keys, top_rate), group),
            head_slots(select_rows(values, top_rate), group),
        ),
        "inner",
        0,
        0,
        1,
    )
    mid_keys = mid_keys_in.reshape(-1, HEAD_DIM)
    mid_values = mid_values_in.reshape(-1, HEAD_DIM)
    top_keys, top_values = sent_together_2(
        (top_keys_in.reshape(-1, HEAD_DIM), top_values_in.reshape(-1, HEAD_DIM)), "outer", 0, 1
    )
    mid_key_slides = slide_index(
        mid_start + jnp.arange(SPARSE, dtype=jnp.int32) * mid_rate + own_head % mid_rate, slide_ends
    )
    top_key_slides = slide_index(
        jnp.arange(SPARSE, dtype=jnp.int32) * top_rate + own_head % top_rate, slide_ends
    )
    mid_query, mid_slides, mid_count = query_slots(
        queries, mid_rate, group, first_token, slide_ends
    )
    top_query, top_slides, top_count = query_slots(
        queries, top_rate, group, first_token, slide_ends
    )
    query_part = lax.all_to_all(mid_query, "inner", split_axis=0, concat_axis=0, tiled=True)
    slide_part = lax.all_to_all(mid_slides, "inner", split_axis=0, concat_axis=0, tiled=True)
    source_count, per_slot = slide_part.shape
    branch, branch_lse = segment_attention(
        query_part.reshape(-1, HEAD_DIM),
        mid_keys,
        mid_values,
        slide_part.reshape(-1),
        mid_key_slides,
    )
    mid_back = unslot(
        (
            lax.all_to_all(
                branch.reshape(source_count, per_slot, HEAD_DIM),
                "inner",
                split_axis=0,
                concat_axis=0,
                tiled=True,
            ),
            lax.all_to_all(
                branch_lse.reshape(source_count, per_slot),
                "inner",
                split_axis=0,
                concat_axis=0,
                tiled=True,
            ),
        ),
        mid_count,
        group,
    )
    query_part = lax.all_to_all(top_query, "inner", split_axis=0, concat_axis=0, tiled=True)
    slide_part = lax.all_to_all(top_slides, "inner", split_axis=0, concat_axis=0, tiled=True)
    source_count, per_slot = slide_part.shape
    branch, branch_lse = segment_attention(
        query_part.reshape(-1, HEAD_DIM),
        top_keys,
        top_values,
        slide_part.reshape(-1),
        top_key_slides,
    )
    top_back = unslot(
        (
            lax.all_to_all(
                branch.reshape(source_count, per_slot, HEAD_DIM),
                "inner",
                split_axis=0,
                concat_axis=0,
                tiled=True,
            ),
            lax.all_to_all(
                branch_lse.reshape(source_count, per_slot),
                "inner",
                split_axis=0,
                concat_axis=0,
                tiled=True,
            ),
        ),
        top_count,
        group,
    )
    for head_index in range(HEADS):
        upper_levels.append(
            (
                spread_rows(
                    mid_back[0][head_index],
                    mid_back[1][head_index],
                    mid_rate,
                    head_index % mid_rate,
                ),
                spread_rows(
                    top_back[0][head_index],
                    top_back[1][head_index],
                    top_rate,
                    head_index % top_rate,
                ),
            )
        )
    head_outputs = []
    for head_index in range(HEADS):
        head_outputs.append(
            mix_levels(
                local_levels[head_index], upper_levels[head_index][0], upper_levels[head_index][1]
            )
        )
    attention = jnp.concatenate(head_outputs, axis=1).astype(jnp.bfloat16)
    return jnp.dot(attention, out_weight, preferred_element_type=jnp.float32).astype(jnp.bfloat16)


def solution(mesh):
    in_specs = (
        P(("outer", "inner"), None),
        P(("outer", "inner"), None),
        P(("outer", "inner"), None),
        P(),
        P(),
    )
    out_specs = P(("outer", "inner"), None)
    return jax.shard_map(shards, mesh=mesh, in_specs=in_specs, out_specs=out_specs, check_vma=False)
```

profile of v0, /device:TPU:1, one launch (start us, length us, event | category | flops | bytes accessed | tf_op | source)
XLA Modules:
  0.0 278.4 jit_solution(17246029246760863815)
XLA Ops:
  0.2 0.7 copy-done.4
  2.1 17.2 %all-to-all-start.4 = ((s32[32,1,1]{2,1,0:T(1,128)}), s32[32,1,1]{2,1,0:T(1,128)S(1)}, u32[]{:S(2)}, u32[]{:S(2)}) async-start(s32[32,1,1]{2,1,0:T(1,128)} %all_to_all.46), calls=%async_computation.4 | async-start | bytes 32768 | tf_op jit(solution)/shard_map/all_to_all | solution.py:238
  19.3 2.1 collective-permute-start
  21.5 2.2 collective-permute-start.2
  23.8 1.1 copy.886
  25.1 0.8 copy-done.3
  25.9 1.1 reshape.1992
  27.0 1.1 reshape.1994
  32.7 1.2 fusion.175
  34.2 1.2 fusion.176
  36.6 1.5 pad_maximum_fusion.1
  38.8 12.2 %all-to-all-start = ((s32[32,1,8]{2,1,0:T(1,128)}), s32[32,1,8]{2,1,0:T(1,128)S(1)}, u32[]{:S(2)}, u32[]{:S(2)}) async-start(s32[32,1,8]{2,1,0:T(1,128)} %bitcast.2), calls=%async_computation | async-start | bytes 32768 | tf_op jit(solution)/shard_map/all_to_all | solution.py:208
  51.0 0.7 reshape.2139
  51.7 11.0 %all-to-all-done = s32[32,1,8]{2,1,0:T(1,128)S(1)} async-done(((s32[32,1,8]{2,1,0:T(1,128)}), s32[32,1,8]{2,1,0:T(1,128)S(1)}, u32[]{:S(2)}, u32[]{:S(2)}) %all-to-all-start) | async-done | bytes 1056 | tf_op jit(solution)/shard_map/all_to_all | solution.py:208
  62.7 4.0 %all-to-all-start.1 = ((bf16[32,2,256]{2,1,0:T(2,128)(2,1)}), bf16[32,2,256]{2,1,0:T(2,128)(2,1)S(1)}, u32[]{:S(2)}, u32[]{:S(2)}) async-start(bf16[32,2,256]{2,1,0:T(2,128)(2,1)} %reshape.2139), calls=%async_computation.1 | async-start | bytes 65536 | tf_op jit(solution)/shard_map/all_to_all | solution.py:207
  66.7 12.1 %all-to-all-done.1 = bf16[32,2,256]{2,1,0:T(2,128)(2,1)S(1)} async-done(((bf16[32,2,256]{2,1,0:T(2,128)(2,1)}), bf16[32,2,256]{2,1,0:T(2,128)(2,1)S(1)}, u32[]{:S(2)}, u32[]{:S(2)}) %all-to-all-start.1) | async-done | bytes 32800 | tf_op jit(solution)/shard_map/all_to_all | solution.py:207
  78.8 3.9 %all-to-all-start.2 = ((bf16[32,68,64]{1,2,0:T(8,128)(2,1)}), bf16[32,68,64]{1,2,0:T(8,128)(2,1)S(1)}, u32[]{:S(2)}, u32[]{:S(2)}) async-start(bf16[32,68,64]{1,2,0:T(8,128)(2,1)} %pad_maximum_fusion.1), calls=%async_computation.2 | async-start | bytes 1048576 | tf_op jit(solution)/shard_map/all_to_all | solution.py:27
  85.6 0.7 compare_reduce_fusion.11
  86.3 0.7 compare_reduce_fusion.10
  87.6 0.7 compare_reduce_fusion.8
  90.4 0.7 compare_reduce_fusion.4
  95.8 1.1 broadcast_select_fusion.5
  96.9 0.8 pad_maximum_fusion
  97.7 7.2 %collective-permute-start.1 = (bf16[512,512]{1,0:T(8,128)(2,1)}, bf16[512,512]{1,0:T(8,128)(2,1)}, u32[]{:S(2)}, u32[]{:S(2)}) collective-permute-start(bf16[512,512]{1,0:T(8,128)(2,1)} %pad_maximum_fusion), channel_id=1, source_target_pairs={{0,2},{2,0},{1,3},{3,1},{4,6},{6,4},{5,7},{7,5},{8,10},{10,8},{9,1... | collective-permute-start | bytes 1572872 | tf_op jit(solution)/shard_map/ppermute | solution.py:21
  104.9 0.9 pad_maximum_fusion.2
  105.7 2.0 collective-permute-start.3
  107.8 12.9 %all-to-all-start.5 = ((bf16[32,1,64]{2,1,0:T(2,128)(2,1)}), bf16[32,1,64]{2,1,0:T(2,128)(2,1)S(1)}, u32[]{:S(2)}, u32[]{:S(2)}) async-start(bf16[32,1,64]{2,1,0:T(2,128)(2,1)} %copy.920), calls=%async_computation.5 | async-start | bytes 32768 | tf_op jit(solution)/shard_map/all_to_all | solution.py:237
  120.6 1.2 fusion.174
  121.8 1.3 copy.921
  123.4 56.0 %all_gather.3 = bf16[1024,128]{1,0:T(8,128)(2,1)S(1)} all-gather(bf16[64,128]{1,0:T(8,128)(2,1)S(1)} %pad_maximum_fusion.7), channel_id=1, replica_groups=mesh['outer'=16,'inner'=32] {'outer'}, dimensions={0}, use_global_device_ids=true | all-gather | bytes 278528 | tf_op jit(solution)/shard_map/all_gather | solution.py:39
  179.9 0.9 convolution_divide_fusion.9
  181.5 16.2 %all-to-all-start.6 = ((f32[32,1,1]{2,1,0:T(1,128)}), f32[32,1,1]{2,1,0:T(1,128)S(1)}, u32[]{:S(2)}, u32[]{:S(2)}) async-start(f32[32,1,1]{2,1,0:T(1,128)} %copy.923), calls=%async_computation.6 | async-start | bytes 32768 | tf_op jit(solution)/shard_map/all_to_all | solution.py:256
  197.7 1.0 fusion.173
  198.7 1.3 copy.906
  201.9 0.8 reshape.2141
  202.7 6.8 %all-to-all-done.6 = f32[32,1,1]{2,1,0:T(1,128)S(1)} async-done(((f32[32,1,1]{2,1,0:T(1,128)}), f32[32,1,1]{2,1,0:T(1,128)S(1)}, u32[]{:S(2)}, u32[]{:S(2)}) %all-to-all-start.6) | async-done | bytes 160 | tf_op jit(solution)/shard_map/all_to_all | solution.py:256
  209.5 5.4 %all-to-all-start.3 = ((f32[32,1,8]{2,1,0:T(1,128)}), f32[32,1,8]{2,1,0:T(1,128)S(1)}, u32[]{:S(2)}, u32[]{:S(2)}) async-start(f32[32,1,8]{2,1,0:T(1,128)} %bitcast.31), calls=%async_computation.3 | async-start | bytes 32768 | tf_op jit(solution)/shard_map/all_to_all | solution.py:226
  215.3 4.9 %fusion.155 = (f32[2,1]{0,1:T(1,128)S(1)}, f32[2,1]{0,1:T(1,128)S(1)}, f32[2,1]{0,1:T(1,128)S(1)}, f32[2,1]{0,1:T(1,128)S(1)}, f32[2,1]{0,1:T(1,128)S(1)}, /*ind...) fusion(pred[]{:T(512)} %compare_reduce_fusion, f32[8,4]{1,0:T(8,128)S(1)} %reshape.2010, ...), kind=kLoop, calls=%fused_computation.386 | loop fusion | flops 16 | bytes 136 | tf_op jit(solution)/shard_map/reshape.1804
  220.9 5.7 %all-to-all-done.3 = f32[32,1,8]{2,1,0:T(1,128)S(1)} async-done(((f32[32,1,8]{2,1,0:T(1,128)}), f32[32,1,8]{2,1,0:T(1,128)S(1)}, u32[]{:S(2)}, u32[]{:S(2)}) %all-to-all-start.3) | async-done | bytes 1056 | tf_op jit(solution)/shard_map/all_to_all | solution.py:226
  226.6 6.4 %all-to-all-start.8 = ((f32[32,1,64]{2,1,0:T(1,128)}), f32[32,1,64]{2,1,0:T(1,128)S(1)}, u32[]{:S(2)}, u32[]{:S(2)}) async-start(f32[32,1,64]{2,1,0:T(1,128)} %bitcast.53), calls=%async_computation.8 | async-start | bytes 32768 | tf_op jit(solution)/shard_map/all_to_all | solution.py:249
  233.1 4.7 %slice_reduce_fusion = (f32[4,8]{1,0:T(4,128)S(1)}, f32[4,8]{1,0:T(4,128)S(1)}, f32[4,8]{1,0:T(4,128)S(1)}, f32[4,8]{1,0:T(4,128)S(1)}, f32[4,8]{1,0:T(4,128)S(1...) fusion(f32[32,1,8]{2,1,0:T(1,128)S(1)} %all-to-all-done.3, pred[]{:T(512)} %compare_reduce_fusion.2, ...), kind=kLoop, calls=%fused_computation.285 | loop fusion | flops 224 | bytes 2055 | tf_op jit(solution)/shard_map/slice | solution.py:272
  239.7 5.1 %all-to-all-done.8 = f32[32,1,64]{2,1,0:T(1,128)S(1)} async-done(((f32[32,1,64]{2,1,0:T(1,128)}), f32[32,1,64]{2,1,0:T(1,128)S(1)}, u32[]{:S(2)}, u32[]{:S(2)}) %all-to-all-start.8) | async-done | bytes 8224 | tf_op jit(solution)/shard_map/all_to_all | solution.py:249
  244.8 7.1 %all-to-all-start.7 = ((f32[32,1,512]{2,1,0:T(1,128)}), f32[32,1,512]{2,1,0:T(1,128)S(1)}, u32[]{:S(2)}, u32[]{:S(2)}) async-start(f32[32,1,512]{2,1,0:T(1,128)} %reshape.2141), calls=%async_computation.7 | async-start | bytes 131072 | tf_op jit(solution)/shard_map/all_to_all | solution.py:219
  253.9 10.1 %all-to-all-done.7 = f32[32,1,512]{2,1,0:T(1,128)S(1)} async-done(((f32[32,1,512]{2,1,0:T(1,128)}), f32[32,1,512]{2,1,0:T(1,128)S(1)}, u32[]{:S(2)}, u32[]{:S(2)}) %all-to-all-start.7) | async-done | bytes 65568 | tf_op jit(solution)/shard_map/all_to_all | solution.py:219
  264.5 0.8 reduce.193
  266.4 1.2 broadcast_select_fusion.2
  273.2 1.2 broadcast_select_fusion
  277.2 1.1 convolution_convert_fusion
  (259 shorter events, 36.3 us)
Async XLA Ops:
  0.0 277.2 %copy-start = (bf16[512,768]{1,0:T(8,128)(2,1)S(1)}, bf16[512,768]{1,0:T(8,128)(2,1)}, u32[]{:S(2)}) copy-start(bf16[512,768]{1,0:T(8,128)(2,1)} %param.72) | copy-start | bytes 2359300
  0.2 0.7 copy-start.4
  2.1 36.7 %all-to-all-start.4 = ((s32[32,1,1]{2,1,0:T(1,128)}), s32[32,1,1]{2,1,0:T(1,128)S(1)}, u32[]{:S(2)}, u32[]{:S(2)}) async-start(s32[32,1,1]{2,1,0:T(1,128)} %all_to_all.46), calls=%async_computation.4 | async-start | bytes 32768 | tf_op jit(solution)/shard_map/all_to_all | solution.py:238
  19.3 76.5 %collective-permute-start = (bf16[256,512]{1,0:T(8,128)(2,1)}, bf16[256,512]{1,0:T(8,128)(2,1)S(1)}, u32[]{:S(2)}, u32[]{:S(2)}) collective-permute-start(bf16[256,512]{1,0:T(8,128)(2,1)} %param.70), channel_id=1, source_target_pairs={{0,1},{1,0},{2,3},{3,2},{4,5},{5,4},{6,7},{7,6},{8,9},{9,8},{10,11... | collective-permute-start | bytes 786440 | tf_op jit(solution)/shard_map/ppermute | solution.py:21
  21.5 74.3 %collective-permute-start.2 = (bf16[256,512]{1,0:T(8,128)(2,1)}, bf16[256,512]{1,0:T(8,128)(2,1)}, u32[]{:S(2)}, u32[]{:S(2)}) collective-permute-start(bf16[256,512]{1,0:T(8,128)(2,1)} %param.71), channel_id=1, source_target_pairs={{0,1},{1,0},{2,3},{3,2},{4,5},{5,4},{6,7},{7,6},{8,9},{9,8},{10,11... | collective-permute-start | bytes 786440 | tf_op jit(solution)/shard_map/ppermute | solution.py:21
  23.8 1.1 copy-start.2
  24.9 1.0 copy-start.3
  27.0 1.1 copy-start.1
  38.8 23.9 %all-to-all-start = ((s32[32,1,8]{2,1,0:T(1,128)}), s32[32,1,8]{2,1,0:T(1,128)S(1)}, u32[]{:S(2)}, u32[]{:S(2)}) async-start(s32[32,1,8]{2,1,0:T(1,128)} %bitcast.2), calls=%async_computation | async-start | bytes 32768 | tf_op jit(solution)/shard_map/all_to_all | solution.py:208
  62.7 16.2 %all-to-all-start.1 = ((bf16[32,2,256]{2,1,0:T(2,128)(2,1)}), bf16[32,2,256]{2,1,0:T(2,128)(2,1)S(1)}, u32[]{:S(2)}, u32[]{:S(2)}) async-start(bf16[32,2,256]{2,1,0:T(2,128)(2,1)} %reshape.2139), calls=%async_computation.1 | async-start | bytes 65536 | tf_op jit(solution)/shard_map/all_to_all | solution.py:207
  78.8 28.9 %all-to-all-start.2 = ((bf16[32,68,64]{1,2,0:T(8,128)(2,1)}), bf16[32,68,64]{1,2,0:T(8,128)(2,1)S(1)}, u32[]{:S(2)}, u32[]{:S(2)}) async-start(bf16[32,68,64]{1,2,0:T(8,128)(2,1)} %pad_maximum_fusion.1), calls=%async_computation.2 | async-start | bytes 1048576 | tf_op jit(solution)/shard_map/all_to_all | solution.py:27
  97.7 168.6 %collective-permute-start.1 = (bf16[512,512]{1,0:T(8,128)(2,1)}, bf16[512,512]{1,0:T(8,128)(2,1)}, u32[]{:S(2)}, u32[]{:S(2)}) collective-permute-start(bf16[512,512]{1,0:T(8,128)(2,1)} %pad_maximum_fusion), channel_id=1, source_target_pairs={{0,2},{2,0},{1,3},{3,1},{4,6},{6,4},{5,7},{7,5},{8,10},{10,8},{9,1... | collective-permute-start | bytes 1572872 | tf_op jit(solution)/shard_map/ppermute | solution.py:21
  105.7 167.4 %collective-permute-start.3 = (bf16[512,512]{1,0:T(8,128)(2,1)}, bf16[512,512]{1,0:T(8,128)(2,1)}, u32[]{:S(2)}, u32[]{:S(2)}) collective-permute-start(bf16[512,512]{1,0:T(8,128)(2,1)} %pad_maximum_fusion.2), channel_id=1, source_target_pairs={{0,2},{2,0},{1,3},{3,1},{4,6},{6,4},{5,7},{7,5},{8,10},{10,8},{9,1... | collective-permute-start | bytes 1572872 | tf_op jit(solution)/shard_map/ppermute | solution.py:21
  107.8 71.7 %all-to-all-start.5 = ((bf16[32,1,64]{2,1,0:T(2,128)(2,1)}), bf16[32,1,64]{2,1,0:T(2,128)(2,1)S(1)}, u32[]{:S(2)}, u32[]{:S(2)}) async-start(bf16[32,1,64]{2,1,0:T(2,128)(2,1)} %copy.920), calls=%async_computation.5 | async-start | bytes 32768 | tf_op jit(solution)/shard_map/all_to_all | solution.py:237
  181.5 28.0 %all-to-all-start.6 = ((f32[32,1,1]{2,1,0:T(1,128)}), f32[32,1,1]{2,1,0:T(1,128)S(1)}, u32[]{:S(2)}, u32[]{:S(2)}) async-start(f32[32,1,1]{2,1,0:T(1,128)} %copy.923), calls=%async_computation.6 | async-start | bytes 32768 | tf_op jit(solution)/shard_map/all_to_all | solution.py:256
  209.5 17.2 %all-to-all-start.3 = ((f32[32,1,8]{2,1,0:T(1,128)}), f32[32,1,8]{2,1,0:T(1,128)S(1)}, u32[]{:S(2)}, u32[]{:S(2)}) async-start(f32[32,1,8]{2,1,0:T(1,128)} %bitcast.31), calls=%async_computation.3 | async-start | bytes 32768 | tf_op jit(solution)/shard_map/all_to_all | solution.py:226
  226.6 18.2 %all-to-all-start.8 = ((f32[32,1,64]{2,1,0:T(1,128)}), f32[32,1,64]{2,1,0:T(1,128)S(1)}, u32[]{:S(2)}, u32[]{:S(2)}) async-start(f32[32,1,64]{2,1,0:T(1,128)} %bitcast.53), calls=%async_computation.8 | async-start | bytes 32768 | tf_op jit(solution)/shard_map/all_to_all | solution.py:249
  244.8 19.2 %all-to-all-start.7 = ((f32[32,1,512]{2,1,0:T(1,128)}), f32[32,1,512]{2,1,0:T(1,128)S(1)}, u32[]{:S(2)}, u32[]{:S(2)}) async-start(f32[32,1,512]{2,1,0:T(1,128)} %reshape.2141), calls=%async_computation.7 | async-start | bytes 131072 | tf_op jit(solution)/shard_map/all_to_all | solution.py:219
where the time goes:
time: 280 us; the launch traced here: 278 us
  starting transfers between devices  98.9 us (35%)
  blocking collectives  56 us (20%)
  waiting for transfers between devices  50.8 us (18%)
  other arithmetic  32.4 us (12%)
  local copies, waits for them, and re-layouts  30.3 us (11%)
  matrix products  8.89 us (3%)
    all_gather x1, blocking collectives, sent_together_2(): filled, at, outs = (lax.all_gather(both, axis, axis=dim, tiled=True), 0, [])  56 us
    all_to_all x2, starting transfers between devices, shards(): lax.all_to_all(branch_lse.reshape(source_count, per_slot), 'inner', split...  21.6 us
    all_to_all x1, starting transfers between devices, shards(): lax.all_to_all(top_slides, 'inner', split_axis=0, concat_axis=0, tiled=True)  17.2 us
    all_to_all x2, waiting for transfers between devices, shards(): lax.all_to_all(branch.reshape(source_count, per_slot, HEAD_DIM), 'inner',...  15.2 us
    another operation x18, other arithmetic  15.2 us
    all_to_all x2, starting transfers between devices, shards(): lax.all_to_all(branch.reshape(source_count, per_slot, HEAD_DIM), 'inner',...  13.5 us
    ppermute x4, starting transfers between devices, from_partner(): return lax.ppermute(block, axis, route)  13.5 us
    all_to_all x1, starting transfers between devices, shards(): lax.all_to_all(top_query, 'inner', split_axis=0, concat_axis=0, tiled=True)  12.9 us
  transfers between devices with their start and end apart: 13, of which 6 were waited for; matrix products, arithmetic and copies ran while one was open for 23% of the time, Pallas kernels for 0%

commit v1 on v0

v1 whole, which is shorter than its diff:
```python
import jax
import jax.numpy as jnp
from jax import lax
from jax.experimental import pallas as pl
from jax.experimental.pallas import tpu as pltpu
from jax.sharding import PartitionSpec as P

HEADS = 8
HEAD_DIM = 64
SPARSE = 1024
SLIDES = 16
TOK = 256
ROWS = 32
MESH = pl.DeviceIdType.MESH
BF = jnp.bfloat16
F32 = jnp.float32

masked_score = -1e30


def iota(shape, dim):
    return lax.broadcasted_iota(jnp.int32, shape, dim)


def nt_dot(a, b):
    return lax.dot_general(a, b, (((1,), (1,)), ((), ())), preferred_element_type=F32)


def nn_dot(a, b):
    return lax.dot_general(a, b, (((1,), (0,)), ((), ())), preferred_element_type=F32)


def one_hot(mask):
    return jnp.where(mask, 1.0, 0.0).astype(BF)


def attend(q, parts, q_ids, k_ids):
    scores = jnp.concatenate([nt_dot(q, kv) for kv in parts], axis=1)
    scores = jnp.where(q_ids == k_ids, scores, masked_score)
    row_max = jnp.max(scores, axis=1, keepdims=True)
    expos = jnp.exp(scores - row_max)
    total = jnp.sum(expos, axis=1, keepdims=True)
    probs = expos.astype(BF)
    mixed, at = None, 0
    for kv in parts:
        term = nn_dot(probs[:, at : at + kv.shape[0]], kv)
        mixed = term if mixed is None else mixed + term
        at += kv.shape[0]
    return mixed / total, row_max + jnp.log(total)


def kernel(
    q_ref, k_ref, v_ref, w_ref, len_ref, out_ref,
    kv, qs, mkv, qmid, topkv, mid_out, top_out, mid_res, top_res, att, diag_o, diag_l,
    ids_q, ids_k,
    s_sib, r_sib, s_yd, r_yd, s_y, r_y, s_fw, r_fw, s_mz, r_mz, s_qz, r_qz,
    s_ty, r_ty, s_tx, r_tx, s_mr, r_mr, s_tr, r_tr,
):
    outer = lax.axis_index("outer")
    inner = lax.axis_index("inner")
    x, y_lo = outer // 4, outer % 4
    z, side, core = inner // 4, (inner // 2) % 2, inner % 2
    y = side * 4 + y_lo

    def at_z(zz, c):
        return (outer, zz * 4 + side * 2 + c)

    def at_xy(xx, yy):
        return (xx * 4 + yy % 4, z * 4 + (yy // 4) * 2 + core)

    def send(src, dst, s, r, device):
        return pltpu.make_async_remote_copy(
            src_ref=src, dst_ref=dst, send_sem=s, recv_sem=r, device_id=device, device_id_type=MESH
        )

    partner = (outer, z * 4 + (1 - side) * 2 + core)
    sibling = at_z(z, 1 - core)
    step2 = 2 - 4 * core
    y_to = [at_xy(x, (y + 1) % 8), at_xy(x, (y + 7) % 8), at_xy(x, (y + 8 + step2) % 8)]
    y_from = [y_to[0], y_to[1], at_xy(x, (y + 8 - step2) % 8)]
    x_to = [at_xy((x + 1) % 4, y), at_xy((x + 3) % 4, y), at_xy((x + 2) % 4, y)]
    z_to = [(z + k) % 8 for k in range(1, 8)]

    barrier = pltpu.get_barrier_semaphore()
    greet = [partner, sibling] + y_from + x_to
    for zz in z_to:
        greet += [at_z(zz, 0), at_z(zz, 1)]
    for device in greet:
        pl.semaphore_signal(barrier, inc=1, device_id=device, device_id_type=MESH)

    row, col = iota((TOK, TOK), 0), iota((TOK, TOK), 1)
    perm = one_hot(col == 8 * (row % ROWS) + row // ROWS)
    low = iota((TOK, 128), 1) < HEAD_DIM
    for p in range(4):
        lanes = slice(p * 128, (p + 1) * 128)
        keys = pltpu.roll(nn_dot(perm, k_ref[:, lanes]), 64, 1)
        vals = nn_dot(perm, v_ref[:, lanes])
        kv[0, 2 * p] = jnp.where(low, vals, keys).astype(BF).reshape(8, ROWS, 128)
        kv[0, 2 * p + 1] = jnp.where(low, keys, vals).astype(BF).reshape(8, ROWS, 128)
    for p in range(4):
        lanes = slice(p * 128, (p + 1) * 128)
        rows = pltpu.roll(nn_dot(perm, q_ref[:, lanes]), 64, 1) * HEAD_DIM**-0.5
        qs[2 * p] = jnp.where(low, 0.0, rows).astype(BF).reshape(8, ROWS, 128)
        qs[2 * p + 1] = jnp.where(low, rows, 0.0).astype(BF).reshape(8, ROWS, 128)

    pl.semaphore_wait(barrier, len(greet))

    slot_own = z * 4 + side * 2 + core
    slot_far = z * 4 + (1 - side) * 2 + core
    for h in range(HEADS):
        send(kv.at[0, h, h], kv.at[2, h, h], s_yd, r_yd, partner).start()
    for zz in z_to:
        for c in (core, 1 - core):
            send(kv.at[0, zz, zz], mkv.at[slot_own], s_mz, r_mz, at_z(zz, c)).start()
        send(qs.at[zz, zz], qmid.at[z], s_qz, r_qz, at_z(zz, core)).start()
    send(kv.at[0, z, z], mkv.at[slot_own], s_mz, r_mz, sibling).start()
    for h in range(HEADS):
        if h > 0:
            send(kv.at[0, h, 0:h], kv.at[2, h, 0:h], s_y.at[h], r_y.at[h], partner).start()
        if h < 7:
            send(kv.at[0, h, h + 1 : 8], kv.at[2, h, h + 1 : 8], s_y.at[h], r_y.at[h], partner).start()
    whole = send(kv.at[0], kv.at[1], s_sib, r_sib, sibling)
    whole.start()
    mkv[slot_own] = kv[0, z, z]
    qmid[z] = qs[z, z]

    ends, running = [], jnp.int32(0)
    for j in range(SLIDES):
        running = running + len_ref[j]
        ends.append(running)

    def slides(positions):
        found = jnp.zeros(positions.shape, jnp.int32)
        for end in ends:
            found = found + (positions >= end).astype(jnp.int32)
        return found

    block = outer * (32 * TOK)
    first = block + inner * TOK
    r = iota((TOK, 1), 0)
    ids_q[...] = jnp.broadcast_to(slides(first + 8 * (r % ROWS) + r // ROWS), (TOK, 128))
    n = iota((1, SPARSE), 1)
    slot, n = n // TOK, n % TOK
    far, other = slot // 2, slot % 2
    device = z * 4 + (side + far - 2 * far * side) * 2 + (core + other - 2 * other * core)
    ids_k[...] = jnp.broadcast_to(
        slides(block + device * TOK + 8 * (n % ROWS) + n // ROWS), (8, SPARSE)
    )

    send(kv.at[0, 0], kv.at[2, 0], s_yd, r_yd, partner).wait_recv()
    for zz in z_to:
        for c in (core, 1 - core):
            send(kv.at[2, zz, zz], mkv.at[slot_far], s_mz, r_mz, at_z(zz, c)).start()
    send(kv.at[2, z, z], mkv.at[slot_far], s_mz, r_mz, sibling).start()
    mkv[slot_far] = kv[2, z, z]
    all_mz = send(mkv.at[0:30], mkv.at[0:30], s_mz, r_mz, sibling)
    all_mz.wait_recv()
    all_qz = send(qmid.at[0:7], qmid.at[0:7], s_qz, r_qz, sibling)
    all_qz.wait_recv()

    mid_kv = mkv[...].reshape(SPARSE, 128)
    mid_q = qmid[...].reshape(TOK, 128)
    row, col = iota((64, SPARSE), 0), iota((64, SPARSE), 1)
    topkv[x, y_lo] = nn_dot(one_hot(col == 16 * row), mid_kv).astype(BF)
    row, col = iota((64, TOK), 0), iota((64, TOK), 1)
    pick = (row % 8 < 2) & (col == row // 8 * ROWS + row % 8 * 16)
    top_q = nn_dot(one_hot(pick), mid_q).astype(BF)
    for device in y_to:
        send(topkv.at[x, y_lo], topkv.at[x, y_lo], s_ty, r_ty, device).start()

    v_low = z % 2
    r, n = iota((TOK, 1), 0), iota((1, SPARSE), 1)
    mid_ids_q = slides(block + ((r // ROWS) * 4 + side * 2 + core) * TOK + 8 * (r % ROWS) + z)
    mid_ids_k = slides(block + (n // ROWS) * TOK + 8 * (n % ROWS) + z)
    branch, branch_lse = attend(mid_q, [mid_kv], mid_ids_q, mid_ids_k)
    holds = iota((TOK, 128), 1) // HEAD_DIM == v_low
    mid_out[...] = jnp.where(holds, branch, branch_lse).reshape(8, ROWS, 128)
    for zz in z_to:
        send(mid_out.at[zz], mid_res.at[z], s_mr, r_mr, at_z(zz, core)).start()
    mid_res[z] = mid_out[z]

    all_ty = send(topkv.at[0, 0:3], topkv.at[0, 0:3], s_ty, r_ty, sibling)
    all_ty.wait_recv()
    for device in x_to:
        send(topkv.at[x], topkv.at[x], s_tx, r_tx, device).start()

    whole.wait_recv()

    def pair(p, _):
        both, lses = [], []
        for e in range(2):
            h = 2 * p + e
            send(kv.at[0, h, 0:7], kv.at[2, h, 0:7], s_y.at[h], r_y.at[h], partner).wait_recv()
            forward = send(kv.at[2, h], kv.at[3, h], s_fw.at[h], r_fw.at[h], sibling)
            forward.start()
            forward.wait_recv()
            parts = [kv[s, h].reshape(TOK, 128) for s in range(4)]
            branch, branch_lse = attend(
                qs[h].reshape(TOK, 128), parts, ids_q[:, 0:1], ids_k[0:1, :]
            )
            diag_o[e] = branch
            diag_l[e] = jnp.broadcast_to(branch_lse, (TOK, 128))
            both.append(branch)
        att[p] = jnp.where(low, both[0], both[1]).astype(BF)
        for e in range(2):
            h = 2 * p + e
            start = pl.multiple_of(h * ROWS, ROWS)
            diag_o[2, pl.ds(start, ROWS)] = diag_o[e, pl.ds(start, ROWS)]
            diag_l[2, pl.ds(start, ROWS)] = diag_l[e, pl.ds(start, ROWS)]
        return _

    lax.fori_loop(0, 1, pair, 0)

    all_tx = send(topkv.at[0:3], topkv.at[0:3], s_tx, r_tx, sibling)
    all_tx.wait_recv()
    r, n = iota((64, 1), 0), iota((1, SPARSE), 1)
    top_ids_q = slides(block + ((r // 8) * 4 + side * 2 + core) * TOK + (r % 8) * 128 + z)
    top_ids_k = slides(n * 128 + z)
    branch, branch_lse = attend(top_q, [topkv[...].reshape(SPARSE, 128)], top_ids_q, top_ids_k)
    holds = iota((64, 128), 1) // HEAD_DIM == v_low
    top_out[...] = jnp.where(holds, branch, branch_lse).reshape(8, 8, 128)
    for zz in z_to:
        send(top_out.at[zz], top_res.at[z], s_tr, r_tr, at_z(zz, core)).start()
    top_res[z] = top_out[z]

    lax.fori_loop(1, 4, pair, 0)

    all_mr = send(mid_out.at[0:7], mid_res.at[0:7], s_mr, r_mr, sibling)
    all_mr.wait_recv()
    all_tr = send(top_out.at[0:7], top_res.at[0:7], s_tr, r_tr, sibling)
    all_tr.wait_recv()
    row = iota((ROWS, 1), 0)
    for h in range(HEADS):
        v_at = h % 2 * HEAD_DIM
        l_at = HEAD_DIM - v_at
        rows = slice(h * ROWS, (h + 1) * ROWS)
        mid, top = mid_res[h], top_res[h]
        top = jnp.where(row == 0, top[0:1], top[1:2])
        lse1 = diag_l[2, rows, 0:1]
        lse2 = mid[:, l_at : l_at + 1]
        lse3 = jnp.where(row % 16 == 0, top[:, l_at : l_at + 1], masked_score)
        largest = jnp.maximum(jnp.maximum(lse1, lse2), lse3)
        f1, f2, f3 = jnp.exp(lse1 - largest), jnp.exp(lse2 - largest), jnp.exp(lse3 - largest)
        mixed = (f1 * diag_o[2, rows] + f2 * mid + f3 * top) / (f1 + f2 + f3)
        att[h // 2, rows, v_at : v_at + HEAD_DIM] = mixed[:, v_at : v_at + HEAD_DIM].astype(BF)
    row, col = iota((TOK, TOK), 0), iota((TOK, TOK), 1)
    back = one_hot(row == 8 * (col % ROWS) + col // ROWS)
    total = None
    for p in range(4):
        rows = nn_dot(back, att[p]).astype(BF)
        term = nn_dot(rows, w_ref[p * 128 : (p + 1) * 128, :])
        total = term if total is None else total + term
    out_ref[...] = total.astype(BF)

    whole.wait_send()
    send(kv.at[0, 0], kv.at[2, 0], s_yd, r_yd, partner).wait_send()
    for h in range(HEADS):
        send(kv.at[0, h, 0:7], kv.at[2, h, 0:7], s_y.at[h], r_y.at[h], partner).wait_send()
        send(kv.at[2, h], kv.at[3, h], s_fw.at[h], r_fw.at[h], sibling).wait_send()
    all_mz.wait_send()
    all_qz.wait_send()
    all_ty.wait_send()
    all_tx.wait_send()
    all_mr.wait_send()
    all_tr.wait_send()


def shards(queries, keys, values, out_weight, slide_lengths):
    vmem = pl.BlockSpec(memory_space=pltpu.VMEM)
    dma = pltpu.SemaphoreType.DMA
    return pl.pallas_call(
        kernel,
        out_shape=jax.ShapeDtypeStruct((TOK, out_weight.shape[1]), BF),
        in_specs=[vmem] * 4 + [pl.BlockSpec(memory_space=pltpu.SMEM)],
        out_specs=vmem,
        scratch_shapes=[
            pltpu.VMEM((4, HEADS, 8, ROWS, 128), BF),
            pltpu.VMEM((HEADS, 8, ROWS, 128), BF),
            pltpu.VMEM((32, ROWS, 128), BF),
            pltpu.VMEM((8, ROWS, 128), BF),
            pltpu.VMEM((4, 4, 64, 128), BF),
            pltpu.VMEM((8, ROWS, 128), F32),
            pltpu.VMEM((8, 8, 128), F32),
            pltpu.VMEM((8, ROWS, 128), F32),
            pltpu.VMEM((8, 8, 128), F32),
            pltpu.VMEM((4, TOK, 128), BF),
            pltpu.VMEM((3, TOK, 128), F32),
            pltpu.VMEM((3, TOK, 128), F32),
            pltpu.VMEM((TOK, 128), jnp.int32),
            pltpu.VMEM((8, SPARSE), jnp.int32),
            dma, dma, dma, dma, dma((8,)), dma((8,)), dma((8,)), dma((8,)),
            dma, dma, dma, dma, dma, dma, dma, dma, dma, dma, dma, dma,
        ],
        compiler_params=pltpu.CompilerParams(
            collective_id=0, has_side_effects=True, vmem_limit_bytes=48 * 1024 * 1024
        ),
        name="dilated",
    )(queries, keys, values, out_weight, slide_lengths)


def solution(mesh):
    rows = P(("outer", "inner"), None)
    return jax.shard_map(
        shards, mesh=mesh, in_specs=(rows, rows, rows, P(), P()), out_specs=rows, check_vma=False
    )
```

time: 280 us -> 63.5 us (0.23)
  starting transfers between devices: 98.9 us -> 0 us
  Pallas kernels: 0 us -> 57.9 us
  blocking collectives: 56 us -> 0 us
  waiting for transfers between devices: 50.8 us -> 0 us
  other arithmetic: 32.4 us -> 0 us
  local copies, waits for them, and re-layouts: 30.3 us -> 5.38 us
  matrix products: 8.89 us -> 0 us
    all_to_all x9 -> x0, starting transfers between devices: 85.4 us -> none  [the longest x2 21.6 us: shards(): lax.all_to_all(branch_lse.reshape(source_count, per_slot), 'inner', split...]
    pallas_call x0 -> x1, Pallas kernels: none -> 57.9 us  [shards(): pl.pallas_call(kernel, out_shape=jax.ShapeDtypeStruct((TOK, out_weight.sh...]
    all_gather x1 -> x0, blocking collectives: 56 us -> none  [sent_together_2(): filled, at, outs = (lax.all_gather(both, axis, axis=dim, tiled=True), 0, [])]
    all_to_all x9 -> x0, waiting for transfers between devices: 50.8 us -> none  [the longest x2 15.2 us: shards(): lax.all_to_all(branch.reshape(source_count, per_slot, HEAD_DIM), 'inner',...]
    another operation x18 -> x0, other arithmetic: 15.2 us -> none
    ppermute x4 -> x0, starting transfers between devices: 13.5 us -> none  [from_partner(): return lax.ppermute(block, axis, route)]
    slice x37 -> x0, local copies, waits for them, and re-layouts: 11.2 us -> none  [the longest x30 5.99 us: select_rows(): grouped[:, head_index % step_rate, head_index, :]]
    dot_general x21 -> x0, matrix products: 8.89 us -> none  [the longest x10 3.92 us: segment_attention(): jnp.dot(probs, value_rows, preferred_element_type=jnp.float32) / totals]
  transfers between devices with their start and end apart: 13 -> 0, of which waited for: 6 -> 0; matrix products, arithmetic and copies ran while one was open for 23% -> 0% of each run, Pallas kernels for 0% -> 0%
where the time goes in v1:
time: 63.5 us; the launch traced here: 63.3 us
  Pallas kernels  57.9 us (91%)
  local copies, waits for them, and re-layouts  5.38 us (8%)
    pallas_call x1, Pallas kernels, shards(): pl.pallas_call(kernel, out_shape=jax.ShapeDtypeStruct((TOK, out_weight.sh...  57.9 us
    unnamed x11, local copies, waits for them, and re-layouts  5.38 us

profile of v1, /device:TPU:1, one launch (start us, length us, event | category | flops | bytes accessed | tf_op | source)
XLA Modules:
  0.0 63.3 jit_solution(11516918729150889258)
XLA Ops:
  0.0 0.0 copy-start
  0.0 1.1 %copy-done = bf16[512,768]{1,0:T(8,128)(2,1)S(1)} copy-done((bf16[512,768]{1,0:T(8,128)(2,1)S(1)}, bf16[512,768]{1,0:T(8,128)(2,1)}, u32[]{:S(2)}) %copy-start) | copy-done | bytes 786456
  1.1 0.0 copy-start.1
  1.1 0.9 %copy-done.1 = bf16[256,512]{1,0:T(8,128)(2,1)S(1)} copy-done((bf16[256,512]{1,0:T(8,128)(2,1)S(1)}, bf16[256,512]{1,0:T(8,128)(2,1)}, u32[]{:S(2)}) %copy-start.1) | copy-done | bytes 262168
  2.1 0.0 copy-start.2
  2.1 0.9 %copy-done.2 = bf16[256,512]{1,0:T(8,128)(2,1)S(1)} copy-done((bf16[256,512]{1,0:T(8,128)(2,1)S(1)}, bf16[256,512]{1,0:T(8,128)(2,1)}, u32[]{:S(2)}) %copy-start.2) | copy-done | bytes 262168
  3.0 0.0 copy-start.3
  3.0 0.9 %copy-done.3 = bf16[256,512]{1,0:T(8,128)(2,1)S(1)} copy-done((bf16[256,512]{1,0:T(8,128)(2,1)S(1)}, bf16[256,512]{1,0:T(8,128)(2,1)}, u32[]{:S(2)}) %copy-start.3) | copy-done | bytes 262168
  4.0 0.0 copy-start.4
  4.0 0.7 %copy-done.4 = s32[16]{0:T(128)S(1)} copy-done((s32[16]{0:T(128)S(1)}, s32[16]{0:T(128)}, u32[]{:S(2)}) %copy-start.4) | copy-done | bytes 88
  4.6 57.9 %dilated.1 = bf16[256,768]{1,0:T(8,128)(2,1)S(1)} custom-call(bf16[256,512]{1,0:T(8,128)(2,1)S(1)} %copy-done.1, bf16[256,512]{1,0:T(8,128)(2,1)S(1)} %copy-done.2, bf16[256,512]{1,0:T(8,128)(2,1)S(1)} %copy-done.3, bf16[512,768]{1,0:T(8,128)(2,1)S(1)} %copy-done, s32[16]{0:T(128)S(1)} %copy-done.4), custom_call_target="tpu_custom_call" | custom-call | tf_op jit(solution)/shard_map/dilated/pallas_call | solution.py:271
  62.5 0.7 %copy.7 = bf16[256,768]{1,0:T(8,128)(2,1)} copy(bf16[256,768]{1,0:T(8,128)(2,1)S(1)} %dilated.1) | data formatting | bytes 786432
Async XLA Ops:
  0.0 1.1 %copy-start = (bf16[512,768]{1,0:T(8,128)(2,1)S(1)}, bf16[512,768]{1,0:T(8,128)(2,1)}, u32[]{:S(2)}) copy-start(bf16[512,768]{1,0:T(8,128)(2,1)} %w_ref.1) | copy-start | bytes 2359300
  1.1 0.9 %copy-start.1 = (bf16[256,512]{1,0:T(8,128)(2,1)S(1)}, bf16[256,512]{1,0:T(8,128)(2,1)}, u32[]{:S(2)}) copy-start(bf16[256,512]{1,0:T(8,128)(2,1)} %q_ref.1) | copy-start | bytes 786436
  2.1 0.9 %copy-start.2 = (bf16[256,512]{1,0:T(8,128)(2,1)S(1)}, bf16[256,512]{1,0:T(8,128)(2,1)}, u32[]{:S(2)}) copy-start(bf16[256,512]{1,0:T(8,128)(2,1)} %k_ref.1) | copy-start | bytes 786436
  3.0 0.9 %copy-start.3 = (bf16[256,512]{1,0:T(8,128)(2,1)S(1)}, bf16[256,512]{1,0:T(8,128)(2,1)}, u32[]{:S(2)}) copy-start(bf16[256,512]{1,0:T(8,128)(2,1)} %v_ref.1) | copy-start | bytes 786436
  4.0 0.7 %copy-start.4 = (s32[16]{0:T(128)S(1)}, s32[16]{0:T(128)}, u32[]{:S(2)}) copy-start(s32[16]{0:T(128)} %len_ref.1) | copy-start | bytes 196

commit v2 on v1

v2 whole, which is shorter than its diff:
```python
import jax
import jax.numpy as jnp
from jax import lax
from jax.experimental import pallas as pl
from jax.experimental.pallas import tpu as pltpu
from jax.sharding import PartitionSpec as P

HEADS = 8
HEAD_DIM = 64
SPARSE = 1024
SLIDES = 16
TOK = 256
FIRST = 1
ROWS = 32
MESH = pl.DeviceIdType.MESH
BF = jnp.bfloat16
F32 = jnp.float32

masked_score = -1e30


def iota(shape, dim):
    return lax.broadcasted_iota(jnp.int32, shape, dim)


def nt_dot(a, b):
    return lax.dot_general(a, b, (((1,), (1,)), ((), ())), preferred_element_type=F32)


def nn_dot(a, b):
    return lax.dot_general(a, b, (((1,), (0,)), ((), ())), preferred_element_type=F32)


def one_hot(mask):
    return jnp.where(mask, 1.0, 0.0).astype(BF)


def attend(q, parts, q_ids, k_ids):
    scores = jnp.concatenate([nt_dot(q, kv) for kv in parts], axis=1)
    scores = jnp.where(q_ids == k_ids, scores, masked_score)
    row_max = jnp.max(scores, axis=1, keepdims=True)
    expos = jnp.exp(scores - row_max)
    total = jnp.sum(expos, axis=1, keepdims=True)
    probs = expos.astype(BF)
    mixed, at = None, 0
    for kv in parts:
        term = nn_dot(probs[:, at : at + kv.shape[0]], kv)
        mixed = term if mixed is None else mixed + term
        at += kv.shape[0]
    return mixed / total, row_max + jnp.log(total)


def kernel(
    q_hbm, k_hbm, v_hbm, w_hbm, len_hbm, out_ref,
    q_ref, k_ref, v_ref, w_ref, len_ref,
    kv, qs, mkv, qmid, t_own, t_y, t_z, topkv, mid_out, top_out, mid_res, top_res,
    mixed, acc, ids_q, ids_k, k_top, v_top,
    ready, loads, s_sib, r_sib, s_yd, r_yd, s_y, r_y, s_fw, r_fw, s_mz, r_mz, s_qz, r_qz,
    s_ty, r_ty, s_tz, r_tz, s_tx, r_tx, s_mr, r_mr, s_tr, r_tr, s_mf, r_mf,
):
    outer = lax.axis_index("outer")
    inner = lax.axis_index("inner")
    x, y_lo = outer // 4, outer % 4
    z, side, core = inner // 4, (inner // 2) % 2, inner % 2
    y = side * 4 + y_lo

    def at_z(zz, c):
        return (outer, zz * 4 + side * 2 + c)

    def at_xy(xx, yy):
        return (xx * 4 + yy % 4, z * 4 + (yy // 4) * 2 + core)

    def send(src, dst, s, r, device):
        return pltpu.make_async_remote_copy(
            src_ref=src, dst_ref=dst, send_sem=s, recv_sem=r, device_id=device, device_id_type=MESH
        )

    partner = at_xy(x, (y + 4) % 8)
    sibling = at_z(z, 1 - core)
    y_to = [at_xy(x, (y + k) % 8) for k in (4, 3, 5, 2, 6, 1, 7)]
    x_to = [at_xy((x + k) % 4, y) for k in (2, 1, 3)]
    z_to = [(z + k) % 8 for k in (4, 3, 5, 2, 6, 1, 7)]

    barrier = pltpu.get_barrier_semaphore()

    def greet(devices):
        for device in devices:
            pl.semaphore_signal(barrier, inc=1, device_id=device, device_id_type=MESH)

    def on_core(device, c):
        return (device[0], device[1] - core + c)

    greet([on_core(device, 0) for device in y_to])

    @pl.when(core == 1)
    def _():
        greet([sibling])

    load = []
    for src, dst in (
        (k_hbm.at[0:16], k_top.at[0]), (k_hbm.at[TOK // 2 : TOK // 2 + 16], k_top.at[1]),
        (v_hbm.at[0:16], v_top.at[0]), (v_hbm.at[TOK // 2 : TOK // 2 + 16], v_top.at[1]),
        (k_hbm, k_ref), (v_hbm, v_ref), (q_hbm, q_ref), (len_hbm, len_ref), (w_hbm, w_ref),
    ):
        load.append(pltpu.make_async_copy(src, dst, loads.at[len(load)]))
        load[-1].start()
    zx_core1 = [at_z(zz, 1) for zz in z_to] + [on_core(device, 1) for device in x_to]
    greet(zx_core1)

    for j in range(4):
        load[j].wait()
    low = iota((32, 128), 1) < HEAD_DIM
    rows = []
    for p in range(4):
        lanes = slice(p * 128, (p + 1) * 128)
        keys = pltpu.roll(k_top[:, :, lanes].reshape(32, 128).astype(F32), 64, 1)
        vals = v_top[:, :, lanes].reshape(32, 128).astype(F32)
        rows += [jnp.where(low, vals, keys).astype(BF), jnp.where(low, keys, vals).astype(BF)]
    row, col = iota((16, TOK), 0), iota((16, TOK), 1)
    pick = one_hot(col == row // 2 * 33 + row % 2 * 16)
    tops = nn_dot(pick, jnp.concatenate(rows, axis=0)).astype(BF)
    t_own[...] = tops
    t_y[y] = tops

    @pl.when(core == 0)
    def _():
        pl.semaphore_wait(barrier, 2 * len(y_to) + 1)
        pl.semaphore_signal(ready, inc=1, device_id=sibling, device_id_type=MESH)

    @pl.when(core == 1)
    def _():
        pl.semaphore_wait(ready, 1)

    for device in y_to:
        send(t_own, t_y.at[y], s_ty, r_ty, device).start()

    row, col = iota((TOK, TOK), 0), iota((TOK, TOK), 1)
    perm = one_hot(col == 8 * (row % ROWS) + row // ROWS)
    low = iota((TOK, 128), 1) < HEAD_DIM
    load[4].wait()
    load[5].wait()
    for p in range(4):
        lanes = slice(p * 128, (p + 1) * 128)
        keys = pltpu.roll(nn_dot(perm, k_ref[:, lanes]), 64, 1)
        vals = nn_dot(perm, v_ref[:, lanes])
        kv[0, 2 * p] = jnp.where(low, vals, keys).astype(BF).reshape(8, ROWS, 128)
        kv[0, 2 * p + 1] = jnp.where(low, keys, vals).astype(BF).reshape(8, ROWS, 128)

    for h in range(HEADS):
        send(kv.at[0, h, h], kv.at[2, h, h], s_yd, r_yd, partner).start()

    def across(h):
        if h > 0:
            send(kv.at[0, h, 0:h], kv.at[2, h, 0:h], s_y.at[h], r_y.at[h], partner).start()
        if h < 7:
            send(kv.at[0, h, h + 1 : 8], kv.at[2, h, h + 1 : 8], s_y.at[h], r_y.at[h], partner).start()

    for h in range(FIRST):
        across(h)
    whole = send(kv.at[0], kv.at[1], s_sib, r_sib, sibling)
    whole.start()

    load[6].wait()
    for p in range(4):
        lanes = slice(p * 128, (p + 1) * 128)
        rows = pltpu.roll(nn_dot(perm, q_ref[:, lanes]), 64, 1) * HEAD_DIM**-0.5
        qs[2 * p] = jnp.where(low, 0.0, rows).astype(BF).reshape(8, ROWS, 128)
        qs[2 * p + 1] = jnp.where(low, rows, 0.0).astype(BF).reshape(8, ROWS, 128)

    load[7].wait()
    ends, running = [], jnp.int32(0)
    for j in range(SLIDES):
        running = running + len_ref[j]
        ends.append(running)

    def slides(positions):
        found = jnp.zeros(positions.shape, jnp.int32)
        for end in ends:
            found = found + (positions >= end).astype(jnp.int32)
        return found

    block = outer * (32 * TOK)
    first = block + inner * TOK
    r = iota((TOK, 1), 0)
    ids_q[...] = jnp.broadcast_to(slides(first + 8 * (r % ROWS) + r // ROWS), (TOK, 128))
    n = iota((1, SPARSE), 1)
    slot, n = n // TOK, n % TOK
    far, other = slot // 2, slot % 2
    device = z * 4 + (side + far - 2 * far * side) * 2 + (core + other - 2 * other * core)
    ids_k[...] = jnp.broadcast_to(
        slides(block + device * TOK + 8 * (n % ROWS) + n // ROWS), (8, SPARSE)
    )

    def own_rows():
        @pl.when(core == 1)
        def _():
            pl.semaphore_wait(barrier, 2 * len(zx_core1))
            pl.semaphore_signal(ready, inc=1, device_id=sibling, device_id_type=MESH)

        @pl.when(core == 0)
        def _():
            pl.semaphore_wait(ready, 1)

        for zz in z_to:
            send(kv.at[0, zz, zz], mkv.at[core, slot_own], s_mz, r_mz, at_z(zz, core)).start()
            send(qs.at[zz, zz], qmid.at[z], s_qz, r_qz, at_z(zz, core)).start()

    slot_own, slot_far = z * 2 + side, z * 2 + 1 - side
    pl.when(z >= 2)(own_rows)

    all_ty = send(t_y.at[0:7], t_y.at[0:7], s_ty, r_ty, sibling)
    all_ty.wait_recv()
    for h in range(FIRST, HEADS):
        across(h)

    row, col = iota((128, 128), 0), iota((128, 128), 1)
    pick = col == row // 2 % 8 * 16 + row // 16 * 2 + row % 2
    t_z[...] = nn_dot(one_hot(pick), t_y[...].reshape(128, 128)).astype(BF).reshape(8, 16, 128)

    pl.when(z < 2)(own_rows)

    slot = z * 2 + core
    for zz in z_to:
        for c in (core, 1 - core):
            send(t_z.at[zz], topkv.at[x, slot], s_tz, r_tz, at_z(zz, c)).start()
    send(t_z.at[z], topkv.at[x, slot], s_tz, r_tz, sibling).start()
    topkv[x, slot] = t_z[z]

    mkv[core, slot_own] = kv[0, z, z]
    qmid[z] = qs[z, z]
    send(kv.at[0, 0], kv.at[2, 0], s_yd, r_yd, partner).wait_recv()
    for zz in z_to:
        send(kv.at[2, zz, zz], mkv.at[core, slot_far], s_mz, r_mz, at_z(zz, core)).start()
    mkv[core, slot_far] = kv[2, z, z]

    def forward(h):
        return send(kv.at[2, h], kv.at[3, h], s_fw.at[h], r_fw.at[h], sibling)

    def arrived(h):
        send(kv.at[0, h, 0:7], kv.at[2, h, 0:7], s_y.at[h], r_y.at[h], partner).wait_recv()
        forward(h).start()

    lane_half = iota((TOK, 128), 1) // HEAD_DIM

    def local(h):
        forward(h).wait_recv()
        parts = [kv[s, h].reshape(TOK, 128) for s in range(4)]
        branch, branch_lse = attend(
            qs[h].reshape(TOK, 128), parts, ids_q[:, 0:1], ids_k[0:1, :]
        )
        mixed[h] = jnp.where(lane_half == h % 2, branch, branch_lse)

    def local_heads(start, stop):
        def body(h, _):
            arrived(h + 1)
            local(h)
            return _

        lax.fori_loop(start, stop, body, 0)

    def mix(h):
        l_at = HEAD_DIM - h % 2 * HEAD_DIM
        rows = slice(h * ROWS, (h + 1) * ROWS)
        row = iota((ROWS, 1), 0)
        own, mid, top = mixed[h, rows, :], mid_res[h], top_res[h]
        top = jnp.where(row == 0, top[0:1], top[1:2])
        lse1 = own[:, l_at : l_at + 1]
        lse2 = mid[:, l_at : l_at + 1]
        lse3 = jnp.where(row % 16 == 0, top[:, l_at : l_at + 1], masked_score)
        largest = jnp.maximum(jnp.maximum(lse1, lse2), lse3)
        f1, f2, f3 = jnp.exp(lse1 - largest), jnp.exp(lse2 - largest), jnp.exp(lse3 - largest)
        mixed[h, rows, :] = (f1 * own + f2 * mid + f3 * top) / (f1 + f2 + f3)

    row, col = iota((TOK, TOK), 0), iota((TOK, TOK), 1)
    back = one_hot(row == 8 * (col % ROWS) + col // ROWS)

    def project(p):
        rows = jnp.where(low, mixed[2 * p], mixed[2 * p + 1]).astype(BF)
        rows = nn_dot(back, rows).astype(BF)
        return nn_dot(rows, w_ref[p * 128 : (p + 1) * 128, :])

    all_tz = send(topkv.at[0, 0:15], topkv.at[0, 0:15], s_tz, r_tz, sibling)
    ahead = (7 - z) // 3
    whole.wait_recv()
    arrived(0)
    local_heads(0, ahead)
    all_tz.wait_recv()
    for device in x_to:
        send(topkv.at[x], topkv.at[x], s_tx, r_tx, device).start()

    all_mz = send(mkv.at[0, 0:14], mkv.at[0, 0:14], s_mz, r_mz, sibling)
    all_mz.wait_recv()
    share = send(mkv.at[core], mkv.at[core], s_mf, r_mf, sibling)
    share.start()
    local_heads(ahead, ahead + 1)
    share.wait_recv()
    all_qz = send(qmid.at[0:7], qmid.at[0:7], s_qz, r_qz, sibling)
    all_qz.wait_recv()
    v_low = z % 2
    mid_q = qmid[...].reshape(TOK, 128)
    r, n = iota((TOK, 1), 0), iota((1, SPARSE), 1)
    mid_ids_q = slides(block + ((r // ROWS) * 4 + side * 2 + core) * TOK + 8 * (r % ROWS) + z)
    slot = n // ROWS
    device = slot % 16 // 2 * 4 + slot % 2 * 2 + slot // 16
    mid_ids_k = slides(block + device * TOK + 8 * (n % ROWS) + z)
    branch, branch_lse = attend(mid_q, [mkv[...].reshape(SPARSE, 128)], mid_ids_q, mid_ids_k)
    holds = iota((TOK, 128), 1) // HEAD_DIM == v_low
    mid_out[...] = jnp.where(holds, branch, branch_lse).reshape(8, ROWS, 128)
    for zz in z_to:
        send(mid_out.at[zz], mid_res.at[z], s_mr, r_mr, at_z(zz, core)).start()
    mid_res[z] = mid_out[z]

    row, col = iota((64, TOK), 0), iota((64, TOK), 1)
    pick = (row % 8 < 2) & (col == row // 8 * ROWS + row % 8 * 16)
    top_q = nn_dot(one_hot(pick), mid_q).astype(BF)
    r, n = iota((64, 1), 0), iota((1, SPARSE), 1)
    top_ids_q = slides(block + ((r // 8) * 4 + side * 2 + core) * TOK + (r % 8) * 128 + z)
    far_y = n // 2 % 8
    device = (n // 256 * 4 + far_y % 4) * 32 + n // 32 % 8 * 4 + far_y // 4 * 2 + n // 16 % 2
    top_ids_k = slides(device * TOK + n % 2 * 128 + z)
    all_tx = send(topkv.at[0:3], topkv.at[0:3], s_tx, r_tx, sibling)
    all_tx.wait_recv()
    branch, branch_lse = attend(top_q, [topkv[...].reshape(SPARSE, 128)], top_ids_q, top_ids_k)
    holds = iota((64, 128), 1) // HEAD_DIM == v_low
    top_out[...] = jnp.where(holds, branch, branch_lse).reshape(8, 8, 128)
    for zz in z_to:
        send(top_out.at[zz], top_res.at[z], s_tr, r_tr, at_z(zz, core)).start()
    top_res[z] = top_out[z]

    local_heads(ahead + 1, 4)
    load[8].wait()
    all_mr = send(mid_out.at[0:7], mid_res.at[0:7], s_mr, r_mr, sibling)
    all_mr.wait_recv()
    all_tr = send(top_out.at[0:7], top_res.at[0:7], s_tr, r_tr, sibling)
    all_tr.wait_recv()
    for h in range(4):
        mix(h)
    acc[...] = project(0) + project(1)
    local_heads(4, 6)
    mix(4)
    mix(5)
    acc[...] += project(2)
    local_heads(6, 7)
    mix(6)
    local(7)
    mix(7)
    out_ref[...] = (acc[...] + project(3)).astype(BF)

    whole.wait_send()
    send(kv.at[0, 0], kv.at[2, 0], s_yd, r_yd, partner).wait_send()
    for h in range(HEADS):
        send(kv.at[0, h, 0:7], kv.at[2, h, 0:7], s_y.at[h], r_y.at[h], partner).wait_send()
        forward(h).wait_send()
    all_mz.wait_send()
    share.wait_send()
    all_qz.wait_send()
    all_ty.wait_send()
    all_tz.wait_send()
    all_tx.wait_send()
    all_mr.wait_send()
    all_tr.wait_send()


def shards(queries, keys, values, out_weight, slide_lengths):
    args = (queries, keys, values, out_weight, slide_lengths)
    dma = pltpu.SemaphoreType.DMA
    width = HEADS * HEAD_DIM
    return pl.pallas_call(
        kernel,
        out_shape=jax.ShapeDtypeStruct((TOK, out_weight.shape[1]), BF),
        in_specs=[pl.BlockSpec(memory_space=pltpu.HBM)] * 5,
        out_specs=pl.BlockSpec(memory_space=pltpu.VMEM),
        scratch_shapes=[
            pltpu.VMEM((TOK, width), BF),
            pltpu.VMEM((TOK, width), BF),
            pltpu.VMEM((TOK, width), BF),
            pltpu.VMEM(out_weight.shape, BF),
            pltpu.SMEM((SLIDES,), jnp.int32),
            pltpu.VMEM((4, HEADS, 8, ROWS, 128), BF),
            pltpu.VMEM((HEADS, 8, ROWS, 128), BF),
            pltpu.VMEM((2, 16, ROWS, 128), BF),
            pltpu.VMEM((8, ROWS, 128), BF),
            pltpu.VMEM((16, 128), BF),
            pltpu.VMEM((8, 16, 128), BF),
            pltpu.VMEM((8, 16, 128), BF),
            pltpu.VMEM((4, 16, 16, 128), BF),
            pltpu.VMEM((8, ROWS, 128), F32),
            pltpu.VMEM((8, 8, 128), F32),
            pltpu.VMEM((8, ROWS, 128), F32),
            pltpu.VMEM((8, 8, 128), F32),
            pltpu.VMEM((HEADS, TOK, 128), F32),
            pltpu.VMEM((TOK, out_weight.shape[1]), F32),
            pltpu.VMEM((TOK, 128), jnp.int32),
            pltpu.VMEM((8, SPARSE), jnp.int32),
            pltpu.VMEM((2, 16, width), BF),
            pltpu.VMEM((2, 16, width), BF),
            pltpu.SemaphoreType.REGULAR, dma((9,)), dma, dma, dma, dma, dma((8,)), dma((8,)), dma((8,)), dma((8,)),
            dma, dma, dma, dma, dma, dma, dma, dma, dma, dma, dma, dma, dma, dma, dma, dma,
        ],
        compiler_params=pltpu.CompilerParams(
            collective_id=0, has_side_effects=True, vmem_limit_bytes=48 * 1024 * 1024
        ),
        name="dilated",
    )(*[pltpu.with_memory_space_constraint(a, pltpu.HBM) for a in args])


def solution(mesh):
    rows = P(("outer", "inner"), None)
    return jax.shard_map(
        shards, mesh=mesh, in_specs=(rows, rows, rows, P(), P()), out_specs=rows, check_vma=False
    )
```

time: 63.5 us -> 45.1 us (0.71)
  Pallas kernels: 57.9 us -> 44.2 us
  local copies, waits for them, and re-layouts: 5.38 us -> 0.75 us
    pallas_call x1, Pallas kernels: 57.9 us -> 44.2 us  [shards(): pl.pallas_call(kernel, out_shape=jax.ShapeDtypeStruct((TOK, out_weight.sh...]
    unnamed x11 -> x1, local copies, waits for them, and re-layouts: 5.38 us -> 0.75 us
where the time goes in v2:
time: 45.1 us; the launch traced here: 44.9 us
  Pallas kernels  44.2 us (98%)
  local copies, waits for them, and re-layouts  0.75 us (2%)
    pallas_call x1, Pallas kernels, shards(): pl.pallas_call(kernel, out_shape=jax.ShapeDtypeStruct((TOK, out_weight.sh...  44.2 us

profile of v2, /device:TPU:1, one launch (start us, length us, event | category | flops | bytes accessed | tf_op | source)
XLA Modules:
  0.0 44.9 jit_solution(13440259132172108539)
XLA Ops:
  0.0 44.2 %dilated.1 = bf16[256,768]{1,0:T(8,128)(2,1)S(1)} custom-call(bf16[256,512]{1,0:T(8,128)(2,1)} %q_hbm.1, bf16[256,512]{1,0:T(8,128)(2,1)} %k_hbm.1, bf16[256,512]{1,0:T(8,128)(2,1)} %v_hbm.1, bf16[512,768]{1,0:T(8,128)(2,1)} %w_hbm.1, s32[16]{0:T(128)} %len_hbm.1), custom_call_target="tpu_custom_call" | custom-call | tf_op jit(solution)/shard_map/dilated/pallas_call | solution.py:368
  44.2 0.7 %copy.7 = bf16[256,768]{1,0:T(8,128)(2,1)} copy(bf16[256,768]{1,0:T(8,128)(2,1)S(1)} %dilated.1) | data formatting | bytes 786432

commit v3 on v2

--- a/solution.py
+++ b/solution.py
@@ -10,7 +10,7 @@
 SPARSE = 1024
 SLIDES = 16
 TOK = 256
-FIRST = 1
+FIRST = 2
 ROWS = 32
 MESH = pl.DeviceIdType.MESH
 BF = jnp.bfloat16
@@ -35,7 +35,7 @@
     return jnp.where(mask, 1.0, 0.0).astype(BF)
 
 
-def attend(q, parts, q_ids, k_ids):
+def attend_part(q, parts, q_ids, k_ids):
     scores = jnp.concatenate([nt_dot(q, kv) for kv in parts], axis=1)
     scores = jnp.where(q_ids == k_ids, scores, masked_score)
     row_max = jnp.max(scores, axis=1, keepdims=True)
@@ -47,14 +47,19 @@
         term = nn_dot(probs[:, at : at + kv.shape[0]], kv)
         mixed = term if mixed is None else mixed + term
         at += kv.shape[0]
+    return mixed, row_max, total
+
+
+def attend(q, parts, q_ids, k_ids):
+    mixed, row_max, total = attend_part(q, parts, q_ids, k_ids)
     return mixed / total, row_max + jnp.log(total)
 
 
 def kernel(
-    q_hbm, k_hbm, v_hbm, w_hbm, len_hbm, out_ref,
-    q_ref, k_ref, v_ref, w_ref, len_ref,
+    q_hbm, k_hbm, v_hbm, len_hbm, out_ref,
+    q_ref, k_ref, v_ref, len_ref,
     kv, qs, mkv, qmid, t_own, t_y, t_z, topkv, mid_out, top_out, mid_res, top_res,
-    mixed, acc, ids_q, ids_k, k_top, v_top,
+    mixed, ids_q, ids_k, k_top, v_top, half_o, half_l,
     ready, loads, s_sib, r_sib, s_yd, r_yd, s_y, r_y, s_fw, r_fw, s_mz, r_mz, s_qz, r_qz,
     s_ty, r_ty, s_tz, r_tz, s_tx, r_tx, s_mr, r_mr, s_tr, r_tr, s_mf, r_mf,
 ):
@@ -100,7 +105,7 @@
     for src, dst in (
         (k_hbm.at[0:16], k_top.at[0]), (k_hbm.at[TOK // 2 : TOK // 2 + 16], k_top.at[1]),
         (v_hbm.at[0:16], v_top.at[0]), (v_hbm.at[TOK // 2 : TOK // 2 + 16], v_top.at[1]),
-        (k_hbm, k_ref), (v_hbm, v_ref), (q_hbm, q_ref), (len_hbm, len_ref), (w_hbm, w_ref),
+        (k_hbm, k_ref), (v_hbm, v_ref), (q_hbm, q_ref), (len_hbm, len_ref),
     ):
         load.append(pltpu.make_async_copy(src, dst, loads.at[len(load)]))
         load[-1].start()
@@ -141,13 +146,27 @@
     load[5].wait()
     for p in range(4):
         lanes = slice(p * 128, (p + 1) * 128)
+        part = perm[p * 64 : (p + 1) * 64]
+        keys = pltpu.roll(nn_dot(part, k_ref[:, lanes]), 64, 1)
+        vals = nn_dot(part, v_ref[:, lanes])
+        kv[0, 2 * p, 2 * p] = jnp.where(low[:32], vals[:32], keys[:32]).astype(BF)
+        kv[0, 2 * p + 1, 2 * p + 1] = jnp.where(low[:32], keys[32:], vals[32:]).astype(BF)
+    for h in range(HEADS):
+        send(kv.at[0, h, h], kv.at[2, h, h], s_yd, r_yd, partner).start()
+
+    def keep(h, rows):
+        rows = rows.astype(BF).reshape(8, ROWS, 128)
+        if h > 0:
+            kv[0, h, 0:h] = rows[0:h]
+        if h < 7:
+            kv[0, h, h + 1 : 8] = rows[h + 1 : 8]
+
+    for p in range(4):
+        lanes = slice(p * 128, (p + 1) * 128)
         keys = pltpu.roll(nn_dot(perm, k_ref[:, lanes]), 64, 1)
         vals = nn_dot(perm, v_ref[:, lanes])
-        kv[0, 2 * p] = jnp.where(low, vals, keys).astype(BF).reshape(8, ROWS, 128)
-        kv[0, 2 * p + 1] = jnp.where(low, keys, vals).astype(BF).reshape(8, ROWS, 128)
-
-    for h in range(HEADS):
-        send(kv.at[0, h, h], kv.at[2, h, h], s_yd, r_yd, partner).start()
+        keep(2 * p, jnp.where(low, vals, keys))
+        keep(2 * p + 1, jnp.where(low, keys, vals))
 
     def across(h):
         if h > 0:
@@ -250,6 +269,11 @@
         )
         mixed[h] = jnp.where(lane_half == h % 2, branch, branch_lse)
 
+    def local_half(h, half):
+        parts = [kv[2 * half + s, h].reshape(TOK, 128) for s in range(2)]
+        keys = slice(half * 2 * TOK, (half + 1) * 2 * TOK)
+        return attend_part(qs[h].reshape(TOK, 128), parts, ids_q[:, 0:1], ids_k[0:1, keys])
+
     def local_heads(start, stop):
         def body(h, _):
             arrived(h + 1)
@@ -262,10 +286,10 @@
         l_at = HEAD_DIM - h % 2 * HEAD_DIM
         rows = slice(h * ROWS, (h + 1) * ROWS)
         row = iota((ROWS, 1), 0)
-        own, mid, top = mixed[h, rows, :], mid_res[h], top_res[h]
+        own, mid, top = mixed[h, rows, :], mid_res[h].astype(F32), top_res[h]
         top = jnp.where(row == 0, top[0:1], top[1:2])
         lse1 = own[:, l_at : l_at + 1]
-        lse2 = mid[:, l_at : l_at + 1]
+        lse2 = mid[:, l_at : l_at + 1] + mid[:, l_at + 1 : l_at + 2] + mid[:, l_at + 2 : l_at + 3]
         lse3 = jnp.where(row % 16 == 0, top[:, l_at : l_at + 1], masked_score)
         largest = jnp.maximum(jnp.maximum(lse1, lse2), lse3)
         f1, f2, f3 = jnp.exp(lse1 - largest), jnp.exp(lse2 - largest), jnp.exp(lse3 - largest)
@@ -274,16 +298,21 @@
     row, col = iota((TOK, TOK), 0), iota((TOK, TOK), 1)
     back = one_hot(row == 8 * (col % ROWS) + col // ROWS)
 
-    def project(p):
+    def restore(p):
         rows = jnp.where(low, mixed[2 * p], mixed[2 * p + 1]).astype(BF)
-        rows = nn_dot(back, rows).astype(BF)
-        return nn_dot(rows, w_ref[p * 128 : (p + 1) * 128, :])
+        out_ref[:, p * 128 : (p + 1) * 128] = nn_dot(back, rows).astype(BF)
 
     all_tz = send(topkv.at[0, 0:15], topkv.at[0, 0:15], s_tz, r_tz, sibling)
-    ahead = (7 - z) // 3
-    whole.wait_recv()
-    arrived(0)
-    local_heads(0, ahead)
+    ahead = (z <= 2).astype(jnp.int32) + (z == 0).astype(jnp.int32)
+    between = jnp.where(z <= 2, ahead + 1, 0)
+    before = 4 + (z <= 3).astype(jnp.int32)
+
+    @pl.when(z <= 2)
+    def _():
+        whole.wait_recv()
+        arrived(0)
+        local_heads(0, ahead)
+
     all_tz.wait_recv()
     for device in x_to:
         send(topkv.at[x], topkv.at[x], s_tx, r_tx, device).start()
@@ -292,7 +321,7 @@
     all_mz.wait_recv()
     share = send(mkv.at[core], mkv.at[core], s_mf, r_mf, sibling)
     share.start()
-    local_heads(ahead, ahead + 1)
+    local_heads(ahead, jnp.maximum(ahead, between))
     share.wait_recv()
     all_qz = send(qmid.at[0:7], qmid.at[0:7], s_qz, r_qz, sibling)
     all_qz.wait_recv()
@@ -305,10 +334,23 @@
     mid_ids_k = slides(block + device * TOK + 8 * (n % ROWS) + z)
     branch, branch_lse = attend(mid_q, [mkv[...].reshape(SPARSE, 128)], mid_ids_q, mid_ids_k)
     holds = iota((TOK, 128), 1) // HEAD_DIM == v_low
-    mid_out[...] = jnp.where(holds, branch, branch_lse).reshape(8, ROWS, 128)
+    third, left = [], branch_lse
+    for _ in range(3):
+        third.append(left.astype(BF).astype(F32))
+        left = left - third[-1]
+    lane = iota((TOK, 128), 1) % HEAD_DIM
+    spread = jnp.where(lane == 0, third[0], jnp.where(lane == 1, third[1], third[2]))
+    mid_out[...] = jnp.where(holds, branch, spread).astype(BF).reshape(8, ROWS, 128)
     for zz in z_to:
         send(mid_out.at[zz], mid_res.at[z], s_mr, r_mr, at_z(zz, core)).start()
     mid_res[z] = mid_out[z]
+
+    @pl.when(z > 2)
+    def _():
+        whole.wait_recv()
+        arrived(0)
+
+    local_heads(between, between + 1)
 
     row, col = iota((64, TOK), 0), iota((64, TOK), 1)
     pick = (row % 8 < 2) & (col == row // 8 * ROWS + row % 8 * 16)
@@ -327,24 +369,35 @@
         send(top_out.at[zz], top_res.at[z], s_tr, r_tr, at_z(zz, core)).start()
     top_res[z] = top_out[z]
 
-    local_heads(ahead + 1, 4)
-    load[8].wait()
+    local_heads(between + 1, before)
     all_mr = send(mid_out.at[0:7], mid_res.at[0:7], s_mr, r_mr, sibling)
     all_mr.wait_recv()
     all_tr = send(top_out.at[0:7], top_res.at[0:7], s_tr, r_tr, sibling)
     all_tr.wait_recv()
     for h in range(4):
         mix(h)
-    acc[...] = project(0) + project(1)
-    local_heads(4, 6)
+    restore(0)
+    restore(1)
+    local_heads(before, 6)
     mix(4)
     mix(5)
-    acc[...] += project(2)
-    local_heads(6, 7)
+    restore(2)
+    near, near_max, near_total = local_half(7, 0)
+    half_o[...] = near
+    half_l[...] = jnp.where(lane_half == 0, near_max, near_total)
+    arrived(7)
+    local(6)
     mix(6)
-    local(7)
+    forward(7).wait_recv()
+    far, far_max, far_total = local_half(7, 1)
+    near_max, near_total = half_l[:, 0:1], half_l[:, HEAD_DIM : HEAD_DIM + 1]
+    row_max = jnp.maximum(near_max, far_max)
+    near_part, far_part = jnp.exp(near_max - row_max), jnp.exp(far_max - row_max)
+    total = near_part * near_total + far_part * far_total
+    branch = (near_part * half_o[...] + far_part * far) / total
+    mixed[7] = jnp.where(lane_half == 1, branch, row_max + jnp.log(total))
     mix(7)
-    out_ref[...] = (acc[...] + project(3)).astype(BF)
+    restore(3)
 
     whole.wait_send()
     send(kv.at[0, 0], kv.at[2, 0], s_yd, r_yd, partner).wait_send()
@@ -362,19 +415,18 @@
 
 
 def shards(queries, keys, values, out_weight, slide_lengths):
-    args = (queries, keys, values, out_weight, slide_lengths)
+    args = (queries, keys, values, slide_lengths)
     dma = pltpu.SemaphoreType.DMA
     width = HEADS * HEAD_DIM
-    return pl.pallas_call(
+    attention = pl.pallas_call(
         kernel,
-        out_shape=jax.ShapeDtypeStruct((TOK, out_weight.shape[1]), BF),
-        in_specs=[pl.BlockSpec(memory_space=pltpu.HBM)] * 5,
+        out_shape=jax.ShapeDtypeStruct((TOK, width), BF),
+        in_specs=[pl.BlockSpec(memory_space=pltpu.HBM)] * 4,
         out_specs=pl.BlockSpec(memory_space=pltpu.VMEM),
         scratch_shapes=[
             pltpu.VMEM((TOK, width), BF),
             pltpu.VMEM((TOK, width), BF),
             pltpu.VMEM((TOK, width), BF),
-            pltpu.VMEM(out_weight.shape, BF),
             pltpu.SMEM((SLIDES,), jnp.int32),
             pltpu.VMEM((4, HEADS, 8, ROWS, 128), BF),
             pltpu.VMEM((HEADS, 8, ROWS, 128), BF),
@@ -384,17 +436,18 @@
             pltpu.VMEM((8, 16, 128), BF),
             pltpu.VMEM((8, 16, 128), BF),
             pltpu.VMEM((4, 16, 16, 128), BF),
-            pltpu.VMEM((8, ROWS, 128), F32),
+            pltpu.VMEM((8, ROWS, 128), BF),
             pltpu.VMEM((8, 8, 128), F32),
-            pltpu.VMEM((8, ROWS, 128), F32),
+            pltpu.VMEM((8, ROWS, 128), BF),
             pltpu.VMEM((8, 8, 128), F32),
             pltpu.VMEM((HEADS, TOK, 128), F32),
-            pltpu.VMEM((TOK, out_weight.shape[1]), F32),
             pltpu.VMEM((TOK, 128), jnp.int32),
             pltpu.VMEM((8, SPARSE), jnp.int32),
             pltpu.VMEM((2, 16, width), BF),
             pltpu.VMEM((2, 16, width), BF),
-            pltpu.SemaphoreType.REGULAR, dma((9,)), dma, dma, dma, dma, dma((8,)), dma((8,)), dma((8,)), dma((8,)),
+            pltpu.VMEM((TOK, 128), F32),
+            pltpu.VMEM((TOK, 128), F32),
+            pltpu.SemaphoreType.REGULAR, dma((8,)), dma, dma, dma, dma, dma((8,)), dma((8,)), dma((8,)), dma((8,)),
             dma, dma, dma, dma, dma, dma, dma, dma, dma, dma, dma, dma, dma, dma, dma, dma,
         ],
         compiler_params=pltpu.CompilerParams(
@@ -402,6 +455,7 @@
         ),
         name="dilated",
     )(*[pltpu.with_memory_space_constraint(a, pltpu.HBM) for a in args])
+    return jnp.dot(attention, out_weight, preferred_element_type=F32).astype(BF)
 
 
 def solution(mesh):

time: 45.1 us -> 41.3 us (0.916)
  Pallas kernels: 44.2 us -> 39.7 us
  matrix products: 0 us -> 1.12 us
  local copies, waits for them, and re-layouts: 0.75 us -> 0.01 us
    pallas_call x1, Pallas kernels: 44.2 us -> 39.7 us  [shards(): pl.pallas_call(kernel, out_shape=jax.ShapeDtypeStruct((TOK, width), BF),...]
    dot_general x0 -> x1, matrix products: none -> 1.12 us  [shards(): return jnp.dot(attention, out_weight, preferred_element_type=F32).astype(BF)]
    unnamed x1 -> x2, local copies, waits for them, and re-layouts: 0.75 us -> 0.01 us
where the time goes in v3:
time: 41.3 us; the launch traced here: 40.9 us
  Pallas kernels  39.7 us (96%)
  matrix products  1.12 us (3%)
    pallas_call x1, Pallas kernels, shards(): pl.pallas_call(kernel, out_shape=jax.ShapeDtypeStruct((TOK, width), BF),...  39.7 us
    dot_general x1, matrix products, shards(): return jnp.dot(attention, out_weight, preferred_element_type=F32).astype(BF)  1.12 us

profile of v3, /device:TPU:1, one launch (start us, length us, event | category | flops | bytes accessed | tf_op | source)
XLA Modules:
  0.0 40.9 jit_solution(670516525532309163)
XLA Ops:
  0.0 0.0 copy-start
  0.0 39.7 %dilated.1 = bf16[256,512]{1,0:T(8,128)(2,1)S(1)} custom-call(bf16[256,512]{1,0:T(8,128)(2,1)} %q_hbm.1, bf16[256,512]{1,0:T(8,128)(2,1)} %k_hbm.1, bf16[256,512]{1,0:T(8,128)(2,1)} %v_hbm.1, s32[16]{0:T(128)} %len_hbm.1), custom_call_target="tpu_custom_call" | custom-call | tf_op jit(solution)/shard_map/dilated/pallas_call | solution.py:421
  39.7 0.0 copy-done
  39.8 1.1 %convolution_convert_fusion = bf16[256,768]{1,0:T(8,128)(2,1)} fusion(bf16[256,512]{1,0:T(8,128)(2,1)S(1)} %dilated.1, bf16[512,768]{1,0:T(8,128)(2,1)S(1)} %copy-done), kind=kOutput, calls=%fused_computation | convolution fusion | flops 201523200 | bytes 1441792 | tf_op jit(solution)/shard_map/dot_general | solution.py:458
Async XLA Ops:
  0.0 39.7 %copy-start = (bf16[512,768]{1,0:T(8,128)(2,1)S(1)}, bf16[512,768]{1,0:T(8,128)(2,1)}, u32[]{:S(2)}) copy-start(bf16[512,768]{1,0:T(8,128)(2,1)} %param.8) | copy-start | bytes 2359300

commit v4 on v3

--- a/solution.py
+++ b/solution.py
@@ -303,15 +303,21 @@
         out_ref[:, p * 128 : (p + 1) * 128] = nn_dot(back, rows).astype(BF)
 
     all_tz = send(topkv.at[0, 0:15], topkv.at[0, 0:15], s_tz, r_tz, sibling)
-    ahead = (z <= 2).astype(jnp.int32) + (z == 0).astype(jnp.int32)
-    between = jnp.where(z <= 2, ahead + 1, 0)
-    before = 4 + (z <= 3).astype(jnp.int32)
+    two = (z == 0) & (x > 0)
+    start = (z <= 2).astype(jnp.int32) + two.astype(jnp.int32)
+    late = z > 3
+    before = 5 - late.astype(jnp.int32)
 
     @pl.when(z <= 2)
     def _():
         whole.wait_recv()
         arrived(0)
-        local_heads(0, ahead)
+        local(0)
+
+    @pl.when(two)
+    def _():
+        arrived(1)
+        local(1)
 
     all_tz.wait_recv()
     for device in x_to:
@@ -321,7 +327,6 @@
     all_mz.wait_recv()
     share = send(mkv.at[core], mkv.at[core], s_mf, r_mf, sibling)
     share.start()
-    local_heads(ahead, jnp.maximum(ahead, between))
     share.wait_recv()
     all_qz = send(qmid.at[0:7], qmid.at[0:7], s_qz, r_qz, sibling)
     all_qz.wait_recv()
@@ -348,9 +353,9 @@
     @pl.when(z > 2)
     def _():
         whole.wait_recv()
-        arrived(0)
-
-    local_heads(between, between + 1)
+
+    arrived(start)
+    local_heads(start, start + 1)
 
     row, col = iota((64, TOK), 0), iota((64, TOK), 1)
     pick = (row % 8 < 2) & (col == row // 8 * ROWS + row % 8 * 16)
@@ -369,7 +374,8 @@
         send(top_out.at[zz], top_res.at[z], s_tr, r_tr, at_z(zz, core)).start()
     top_res[z] = top_out[z]
 
-    local_heads(between + 1, before)
+    local_heads(start + 1, before)
+    local(before)
     all_mr = send(mid_out.at[0:7], mid_res.at[0:7], s_mr, r_mr, sibling)
     all_mr.wait_recv()
     all_tr = send(top_out.at[0:7], top_res.at[0:7], s_tr, r_tr, sibling)
@@ -378,7 +384,13 @@
         mix(h)
     restore(0)
     restore(1)
-    local_heads(before, 6)
+
+    @pl.when(late)
+    def _():
+        arrived(5)
+        local(5)
+
+    arrived(6)
     mix(4)
     mix(5)
     restore(2)

time: 41.3 us -> 40.6 us (0.983)
  Pallas kernels: 39.7 us -> 39.1 us
    pallas_call x1, Pallas kernels: 39.7 us -> 39.1 us  [shards(): pl.pallas_call(kernel, out_shape=jax.ShapeDtypeStruct((TOK, width), BF),...]
where the time goes in v4:
time: 40.6 us; the launch traced here: 40.3 us
  Pallas kernels  39.1 us (96%)
  matrix products  1.12 us (3%)
    pallas_call x1, Pallas kernels, shards(): pl.pallas_call(kernel, out_shape=jax.ShapeDtypeStruct((TOK, width), BF),...  39.1 us
    dot_general x1, matrix products, shards(): return jnp.dot(attention, out_weight, preferred_element_type=F32).astype(BF)  1.12 us

profile of v4, /device:TPU:1, one launch (start us, length us, event | category | flops | bytes accessed | tf_op | source)
XLA Modules:
  0.0 40.3 jit_solution(13677270419472382791)
XLA Ops:
  0.0 0.0 copy-start
  0.0 39.1 %dilated.1 = bf16[256,512]{1,0:T(8,128)(2,1)S(1)} custom-call(bf16[256,512]{1,0:T(8,128)(2,1)} %q_hbm.1, bf16[256,512]{1,0:T(8,128)(2,1)} %k_hbm.1, bf16[256,512]{1,0:T(8,128)(2,1)} %v_hbm.1, s32[16]{0:T(128)} %len_hbm.1), custom_call_target="tpu_custom_call" | custom-call | tf_op jit(solution)/shard_map/dilated/pallas_call | solution.py:433
  39.1 0.0 copy-done
  39.2 1.1 %convolution_convert_fusion = bf16[256,768]{1,0:T(8,128)(2,1)} fusion(bf16[256,512]{1,0:T(8,128)(2,1)S(1)} %dilated.1, bf16[512,768]{1,0:T(8,128)(2,1)S(1)} %copy-done), kind=kOutput, calls=%fused_computation | convolution fusion | flops 201523200 | bytes 1441792 | tf_op jit(solution)/shard_map/dot_general | solution.py:470
Async XLA Ops:
  0.0 39.1 %copy-start = (bf16[512,768]{1,0:T(8,128)(2,1)S(1)}, bf16[512,768]{1,0:T(8,128)(2,1)}, u32[]{:S(2)}) copy-start(bf16[512,768]{1,0:T(8,128)(2,1)} %param.8) | copy-start | bytes 2359300

commit v5 on v4

--- a/solution.py
+++ b/solution.py
@@ -35,7 +35,7 @@
     return jnp.where(mask, 1.0, 0.0).astype(BF)
 
 
-def attend_part(q, parts, q_ids, k_ids):
+def attend(q, parts, q_ids, k_ids):
     scores = jnp.concatenate([nt_dot(q, kv) for kv in parts], axis=1)
     scores = jnp.where(q_ids == k_ids, scores, masked_score)
     row_max = jnp.max(scores, axis=1, keepdims=True)
@@ -47,11 +47,6 @@
         term = nn_dot(probs[:, at : at + kv.shape[0]], kv)
         mixed = term if mixed is None else mixed + term
         at += kv.shape[0]
-    return mixed, row_max, total
-
-
-def attend(q, parts, q_ids, k_ids):
-    mixed, row_max, total = attend_part(q, parts, q_ids, k_ids)
     return mixed / total, row_max + jnp.log(total)
 
 
@@ -59,7 +54,7 @@
     q_hbm, k_hbm, v_hbm, len_hbm, out_ref,
     q_ref, k_ref, v_ref, len_ref,
     kv, qs, mkv, qmid, t_own, t_y, t_z, topkv, mid_out, top_out, mid_res, top_res,
-    mixed, ids_q, ids_k, k_top, v_top, half_o, half_l,
+    mixed, ids_q, ids_k, k_top, v_top,
     ready, loads, s_sib, r_sib, s_yd, r_yd, s_y, r_y, s_fw, r_fw, s_mz, r_mz, s_qz, r_qz,
     s_ty, r_ty, s_tz, r_tz, s_tx, r_tx, s_mr, r_mr, s_tr, r_tr, s_mf, r_mf,
 ):
@@ -269,11 +264,6 @@
         )
         mixed[h] = jnp.where(lane_half == h % 2, branch, branch_lse)
 
-    def local_half(h, half):
-        parts = [kv[2 * half + s, h].reshape(TOK, 128) for s in range(2)]
-        keys = slice(half * 2 * TOK, (half + 1) * 2 * TOK)
-        return attend_part(qs[h].reshape(TOK, 128), parts, ids_q[:, 0:1], ids_k[0:1, keys])
-
     def local_heads(start, stop):
         def body(h, _):
             arrived(h + 1)
@@ -286,10 +276,10 @@
         l_at = HEAD_DIM - h % 2 * HEAD_DIM
         rows = slice(h * ROWS, (h + 1) * ROWS)
         row = iota((ROWS, 1), 0)
-        own, mid, top = mixed[h, rows, :], mid_res[h].astype(F32), top_res[h]
+        own, mid, top = mixed[h, rows, :], mid_res[h], top_res[h]
         top = jnp.where(row == 0, top[0:1], top[1:2])
         lse1 = own[:, l_at : l_at + 1]
-        lse2 = mid[:, l_at : l_at + 1] + mid[:, l_at + 1 : l_at + 2] + mid[:, l_at + 2 : l_at + 3]
+        lse2 = mid[:, l_at : l_at + 1]
         lse3 = jnp.where(row % 16 == 0, top[:, l_at : l_at + 1], masked_score)
         largest = jnp.maximum(jnp.maximum(lse1, lse2), lse3)
         f1, f2, f3 = jnp.exp(lse1 - largest), jnp.exp(lse2 - largest), jnp.exp(lse3 - largest)
@@ -339,13 +329,7 @@
     mid_ids_k = slides(block + device * TOK + 8 * (n % ROWS) + z)
     branch, branch_lse = attend(mid_q, [mkv[...].reshape(SPARSE, 128)], mid_ids_q, mid_ids_k)
     holds = iota((TOK, 128), 1) // HEAD_DIM == v_low
-    third, left = [], branch_lse
-    for _ in range(3):
-        third.append(left.astype(BF).astype(F32))
-        left = left - third[-1]
-    lane = iota((TOK, 128), 1) % HEAD_DIM
-    spread = jnp.where(lane == 0, third[0], jnp.where(lane == 1, third[1], third[2]))
-    mid_out[...] = jnp.where(holds, branch, spread).astype(BF).reshape(8, ROWS, 128)
+    mid_out[...] = jnp.where(holds, branch, branch_lse).reshape(8, ROWS, 128)
     for zz in z_to:
         send(mid_out.at[zz], mid_res.at[z], s_mr, r_mr, at_z(zz, core)).start()
     mid_res[z] = mid_out[z]
@@ -394,20 +378,10 @@
     mix(4)
     mix(5)
     restore(2)
-    near, near_max, near_total = local_half(7, 0)
-    half_o[...] = near
-    half_l[...] = jnp.where(lane_half == 0, near_max, near_total)
     arrived(7)
     local(6)
     mix(6)
-    forward(7).wait_recv()
-    far, far_max, far_total = local_half(7, 1)
-    near_max, near_total = half_l[:, 0:1], half_l[:, HEAD_DIM : HEAD_DIM + 1]
-    row_max = jnp.maximum(near_max, far_max)
-    near_part, far_part = jnp.exp(near_max - row_max), jnp.exp(far_max - row_max)
-    total = near_part * near_total + far_part * far_total
-    branch = (near_part * half_o[...] + far_part * far) / total
-    mixed[7] = jnp.where(lane_half == 1, branch, row_max + jnp.log(total))
+    local(7)
     mix(7)
     restore(3)
 
@@ -448,17 +422,15 @@
             pltpu.VMEM((8, 16, 128), BF),
             pltpu.VMEM((8, 16, 128), BF),
             pltpu.VMEM((4, 16, 16, 128), BF),
-            pltpu.VMEM((8, ROWS, 128), BF),
+            pltpu.VMEM((8, ROWS, 128), F32),
             pltpu.VMEM((8, 8, 128), F32),
-            pltpu.VMEM((8, ROWS, 128), BF),
+            pltpu.VMEM((8, ROWS, 128), F32),
             pltpu.VMEM((8, 8, 128), F32),
             pltpu.VMEM((HEADS, TOK, 128), F32),
             pltpu.VMEM((TOK, 128), jnp.int32),
             pltpu.VMEM((8, SPARSE), jnp.int32),
             pltpu.VMEM((2, 16, width), BF),
             pltpu.VMEM((2, 16, width), BF),
-            pltpu.VMEM((TOK, 128), F32),
-            pltpu.VMEM((TOK, 128), F32),
             pltpu.SemaphoreType.REGULAR, dma((8,)), dma, dma, dma, dma, dma((8,)), dma((8,)), dma((8,)), dma((8,)),
             dma, dma, dma, dma, dma, dma, dma, dma, dma, dma, dma, dma, dma, dma, dma, dma,
         ],

time: 40.6 us -> 40.3 us (level)
  no operation moved by 1% of the time
where the time goes in v5:
time: 40.3 us; the launch traced here: 40 us
  Pallas kernels  38.9 us (97%)
  matrix products  1.12 us (3%)
    pallas_call x1, Pallas kernels, shards(): pl.pallas_call(kernel, out_shape=jax.ShapeDtypeStruct((TOK, width), BF),...  38.9 us
    dot_general x1, matrix products, shards(): return jnp.dot(attention, out_weight, preferred_element_type=F32).astype(BF)  1.12 us

profile of v5, /device:TPU:1, one launch (start us, length us, event | category | flops | bytes accessed | tf_op | source)
XLA Modules:
  0.0 40.0 jit_solution(2118875785305633926)
XLA Ops:
  0.0 0.0 copy-start
  0.0 38.9 %dilated.1 = bf16[256,512]{1,0:T(8,128)(2,1)S(1)} custom-call(bf16[256,512]{1,0:T(8,128)(2,1)} %q_hbm.1, bf16[256,512]{1,0:T(8,128)(2,1)} %k_hbm.1, bf16[256,512]{1,0:T(8,128)(2,1)} %v_hbm.1, s32[16]{0:T(128)} %len_hbm.1), custom_call_target="tpu_custom_call" | custom-call | tf_op jit(solution)/shard_map/dilated/pallas_call | solution.py:407
  38.9 0.0 copy-done
  38.9 1.1 %convolution_convert_fusion = bf16[256,768]{1,0:T(8,128)(2,1)} fusion(bf16[256,512]{1,0:T(8,128)(2,1)S(1)} %dilated.1, bf16[512,768]{1,0:T(8,128)(2,1)S(1)} %copy-done), kind=kOutput, calls=%fused_computation | convolution fusion | flops 201523200 | bytes 1441792 | tf_op jit(solution)/shard_map/dot_general | solution.py:442
Async XLA Ops:
  0.0 38.9 %copy-start = (bf16[512,768]{1,0:T(8,128)(2,1)S(1)}, bf16[512,768]{1,0:T(8,128)(2,1)}, u32[]{:S(2)}) copy-start(bf16[512,768]{1,0:T(8,128)(2,1)} %param.8) | copy-start | bytes 2359300
